TPU v7x, 32 devices: a whole 2x2x4 slice. The times are simulated.
32 devices in a mesh: cfd: 16 (over z, x, core), ac: 2 (over y).
Axes of the slice: x: 2, y: 2, z: 4, core: 2. Of those that a mesh axis runs over, the one named last changes fastest.
Arguments:
- surface_raw: bfloat16 [5, 4096, 1024], P(None, ('cfd', 'ac')), may hold values from -6 to 6
- area_normals: bfloat16 [3, 4096], P(None, ('cfd', 'ac')), may hold values from -6 to 6
- kernel_weights: bfloat16 [2, 3, 2048, 4096], P(None, None, None, ('cfd', 'ac')), may hold values from -0.078125 to 0.078125
- block_map: int32 [2, 16, 16], P('ac', 'cfd'), may hold values from 0 to 15, as said below
- band_observers: int32 [16, 128], replicated, may hold values from 0 to 2047, as said below
- band_lags: int32 [16], replicated, may hold values from 0 to 511
Outputs:
- acoustic: float32 [2048, 512], P('cfd', 'ac')
Inputs may be any that keep to these rules, and one draw needn't show every extreme that they name: block_map[j, s, :] is a permutation of 0 to 15 for every j and s. `band_observers`: every observer appears exactly once.
All inputs are finite; a program needn't handle non-finite values.
Results may differ from a plain program's by a relative error of at most 0.0042.
Values may be sent and summed in bfloat16 or wider, within the bound.
A program may use at most 64 MiB of HBM per device.

v0:
```python
import functools

import jax
import jax.numpy as jnp
from jax import lax
from jax.experimental import pallas as pl
from jax.experimental.pallas import tpu as pltpu
from jax.sharding import PartitionSpec as P

LANES = 128


def prepare_kernel(src_ref, normals_ref, surface_ref, out_ref):
    along = surface_ref[2].astype(jnp.float32) * normals_ref[:, 0:1]
    along = along + surface_ref[3].astype(jnp.float32) * normals_ref[:, 1:2]
    along = along + surface_ref[4].astype(jnp.float32) * normals_ref[:, 2:3]
    thick = (surface_ref[1].astype(jnp.float32) * along).astype(jnp.bfloat16)
    both = jnp.concatenate([thick, surface_ref[0]], axis=0)
    rows = both.shape[0]
    column = lax.broadcasted_iota(jnp.int32, (rows, rows), 1)
    onehot = jnp.where(column == src_ref[...], 1.0, 0.0).astype(jnp.bfloat16)
    picked = jnp.dot(onehot, both, preferred_element_type=jnp.float32)
    out_ref[...] = picked.astype(jnp.bfloat16)


def prepare(surface_raw, area_normals, block_order):
    faces, steps = surface_raw.shape[1:]
    blocks = block_order.shape[0]
    size = faces // blocks
    src = (
        jnp.arange(2, dtype=jnp.int32)[None, :, None] * faces
        + block_order[:, None, None] * size
        + jnp.arange(size, dtype=jnp.int32)[None, None, :]
    ).reshape(2 * faces, 1)
    return pl.pallas_call(
        prepare_kernel,
        out_shape=jax.ShapeDtypeStruct((2 * faces, steps), jnp.bfloat16),
        name="prepare",
    )(src, area_normals.T.astype(jnp.float32), surface_raw)


def scatter_bands(lags_ref, ids_ref, arrived_ref, weights_ref, sources, band, rows):
    index = pl.program_id(0)
    taps, terms, width, faces = weights_ref.shape
    steps = sources.shape[1]
    out_len = steps // 2
    chunks = out_len // LANES

    @pl.when(index == 0)
    def _():
        series = arrived_ref[...].astype(jnp.float32)
        if len(arrived_ref.shape) == 4:
            thick = series[:, 0].reshape(faces, steps)
            pressure = series[:, 1].reshape(faces, steps)
        else:
            thick, pressure = series[:faces], series[faces:]
        step = lax.broadcasted_iota(jnp.int32, (faces, steps), 1)

        def rate(x):
            moved = jnp.where(step > 0, x - pltpu.roll(x, 1, 1), 0.0)
            return moved.astype(jnp.bfloat16).astype(jnp.float32)

        for c, x in enumerate((rate(thick), rate(pressure), pressure)):
            for k in range(taps):
                late = pltpu.roll(x, k, 1) if k else x
                sources[pl.ds((k * terms + c) * faces, faces), :] = late.astype(jnp.bfloat16)

    start = out_len - lags_ref[index]
    tile = jnp.minimum(start // LANES, steps // LANES - chunks - 1)
    rest = start - tile * LANES
    shift = lax.rem(LANES - rest, LANES)
    chosen = jnp.concatenate(
        [weights_ref[k, c] for k in range(taps) for c in range(terms)], axis=1
    )
    window = sources[:, pl.ds(pl.multiple_of(tile * LANES, LANES), out_len + LANES)]
    wide = jnp.dot(chosen, window, preferred_element_type=jnp.float32)
    lane = lax.broadcasted_iota(jnp.int32, (width, LANES), 1)
    parts = [
        pltpu.roll(wide[:, t * LANES : (t + 1) * LANES], shift, 1) for t in range(chunks + 1)
    ]
    for t in range(chunks):
        band[pl.ds(t, width, stride=chunks), :] = jnp.where(
            lane < LANES - rest, parts[t], parts[t + 1]
        )

    unroll = 32

    @pl.loop(0, width // unroll)
    def _(group):
        slots = [group * unroll + m for m in range(unroll)]
        places = [ids_ref[index * width + slot] for slot in slots]
        values = [
            band[pl.ds(pl.multiple_of(slot * chunks, chunks), chunks), :] for slot in slots
        ]
        for place, value in zip(places, values):
            rows[pl.ds(pl.multiple_of(place * chunks, chunks), chunks), :] = value


def halves_kernel(
    lags_ref, ids_ref, mine_ref, arrived_ref, weights_ref, kept_ref, sent_ref, sources, band, rows
):
    scatter_bands(lags_ref, ids_ref, arrived_ref, weights_ref, sources, band, rows)
    pairs, height, out_len = kept_ref.shape
    chunks = out_len // LANES
    mine = mine_ref[0]

    @pl.when(pl.program_id(0) == pl.num_programs(0) - 1)
    def _():
        for pair in range(pairs):
            for t in range(chunks):
                lanes = slice(t * LANES, (t + 1) * LANES)
                for out, owner in ((kept_ref, 2 * pair + mine), (sent_ref, 2 * pair + 1 - mine)):
                    first = pl.multiple_of(owner * (height * chunks), height * chunks)
                    part = rows[pl.ds(first + t, height, stride=chunks), :]
                    out[pair, :, lanes] = part.astype(out.dtype)


def banded_call(kernel, outs, arrived, kernel_weights, band_observers, band_lags, mine):
    taps, terms, observers, faces = kernel_weights.shape
    bands, width = band_observers.shape
    steps = arrived.shape[-1]
    chunks = steps // 2 // LANES
    rank = len(arrived.shape)
    return pl.pallas_call(
        kernel,
        out_shape=outs,
        grid_spec=pltpu.PrefetchScalarGridSpec(
            num_scalar_prefetch=3,
            grid=(bands,),
            in_specs=[
                pl.BlockSpec(arrived.shape, lambda b, *_: (0,) * rank),
                pl.BlockSpec((taps, terms, width, faces), lambda b, *_: (0, 0, b, 0)),
            ],
            out_specs=jax.tree.map(
                lambda o: pl.BlockSpec(o.shape, lambda b, *_: (0,) * len(o.shape)), outs
            ),
            scratch_shapes=[
                pltpu.VMEM((taps * terms * faces, steps), jnp.bfloat16),
                pltpu.VMEM((width * chunks, LANES), jnp.float32),
                pltpu.VMEM((observers * chunks, LANES), jnp.float32),
            ],
        ),
        compiler_params=pltpu.CompilerParams(dimension_semantics=("arbitrary",)),
        name="bands",
    )(band_lags, band_observers.reshape(-1), mine, arrived, kernel_weights)


def halve(total, axis, bit):
    size = lax.axis_size(axis)
    mine = (lax.axis_index(axis) >> bit) & 1
    if axis == "cfd":
        owners, rows, times = total.shape
        pairs = total.reshape(owners // 2, 2, rows, times)
        first, second = pairs[:, 0], pairs[:, 1]
    else:
        first, second = jnp.split(total, 2, axis=2)
    kept = jnp.where(mine == 1, second, first)
    sent = jnp.where(mine == 1, first, second).astype(jnp.bfloat16)
    partners = [(i, i ^ (1 << bit)) for i in range(size)]
    return kept + lax.ppermute(sent, axis, partners).astype(jnp.float32)


def exchange_sums(kept, sent):
    owners = lax.axis_size("cfd")
    near = [("cfd", b) for b in range(owners.bit_length() - 1)]
    across = [("ac", b) for b in reversed(range(lax.axis_size("ac").bit_length() - 1))]
    orders = (near[:2] + across + near[2:], near[:1] + across + near[1:])
    partners = [(i, i ^ 1) for i in range(owners)]
    total = kept + lax.ppermute(sent, "cfd", partners).astype(jnp.float32)
    streams = jnp.split(total, len(orders), axis=1)
    for step in range(1, len(near) + len(across)):
        streams = [halve(part, *order[step]) for part, order in zip(streams, orders)]
    return jnp.concatenate([part[0] for part in streams], axis=0)


def local(surface_raw, area_normals, kernel_weights, block_map, band_observers, band_lags):
    blocks = lax.axis_size("cfd")
    faces, steps = surface_raw.shape[1:]
    size = faces // blocks
    outgoing = prepare(surface_raw, area_normals, block_map[0, 0])
    arrived = lax.all_to_all(outgoing, "cfd", split_axis=0, concat_axis=0, tiled=True)
    arrived = arrived.reshape(blocks, 2, size, steps)
    if size % 8:
        arrived = arrived.transpose(1, 0, 2, 3).reshape(2 * faces, steps)
    shape = (blocks // 2, kernel_weights.shape[2] // blocks, steps // 2)
    kept, sent = banded_call(
        halves_kernel,
        [jax.ShapeDtypeStruct(shape, kind) for kind in (jnp.float32, jnp.bfloat16)],
        arrived,
        kernel_weights,
        band_observers,
        band_lags,
        (lax.axis_index("cfd") & 1).astype(jnp.int32).reshape(1),
    )
    return exchange_sums(kept, sent)


def solution(mesh):
    placed = (
        P(None, ("cfd", "ac"), None),
        P(None, ("cfd", "ac")),
        P(None, None, None, ("cfd", "ac")),
        P("ac", "cfd", None),
        P(),
        P(),
    )
    return jax.shard_map(
        local, mesh=mesh, in_specs=placed, out_specs=P("cfd", "ac"), check_vma=False
    )
```

profile of v0, /device:TPU:0, one launch (start us, length us, event | category | flops | bytes accessed | tf_op | source)
XLA Modules:
  0.0 76.9 jit_solution(6417355379833056607)
XLA Ops:
  0.0 0.7 multiply_bitcast_fusion
  0.7 0.1 broadcast_add_fusion
  0.7 0.1 iota_add_fusion
  0.8 0.8 add.84.src_ref
  1.6 1.4 %copy.16 = f32[3,128]{0,1:T(8,128)} copy(bf16[3,128]{1,0:T(4,128)(2,1)} %param.7) | data formatting | bytes 2304 | tf_op jit(solution)/shard_map/convert_element_type | solution.py:39
  3.0 2.7 %prepare.1 = bf16[256,1024]{1,0:T(8,128)(2,1)} custom-call(s32[256,1]{1,0:T(8,128)} %add.84.src_ref, f32[128,3]{1,0:T(8,128)} %bitcast.127, bf16[5,128,1024]{2,1,0:T(8,128)(2,1)} %surface_ref.1), custom_call_target="tpu_custom_call" | custom-call | tf_op jit(solution)/shard_map/prepare/pallas_call | solution.py:35
  5.7 7.4 %all-to-all-start = ((bf16[16,16,1024]{2,1,0:T(8,128)(2,1)}), bf16[16,16,1024]{2,1,0:T(8,128)(2,1)S(1)}, u32[]{:S(2)}, u32[]{:S(2)}) async-start(bf16[16,16,1024]{2,1,0:T(8,128)(2,1)} %bitcast.122), calls=%async_computation | async-start | bytes 1048576 | tf_op jit(solution)/shard_map/all_to_all | solution.py:181
  13.1 14.3 %all-to-all-done = bf16[16,16,1024]{2,1,0:T(8,128)(2,1)S(1)} async-done(((bf16[16,16,1024]{2,1,0:T(8,128)(2,1)}), bf16[16,16,1024]{2,1,0:T(8,128)(2,1)S(1)}, u32[]{:S(2)}, u32[]{:S(2)}) %all-to-all-start) | async-done | bytes 524320 | tf_op jit(solution)/shard_map/all_to_all | solution.py:181
  27.4 0.0 copy-start
  27.4 0.8 %copy-done = bf16[16,16,1024]{2,1,0:T(8,128)(2,1)} copy-done((bf16[16,16,1024]{2,1,0:T(8,128)(2,1)}, bf16[16,16,1024]{2,1,0:T(8,128)(2,1)S(1)}, u32[]{:S(2)}) %copy-start) | copy-done | bytes 524312
  28.2 16.7 %bands.1 = (f32[8,128,512]{2,1,0:T(8,128)}, bf16[8,128,512]{2,1,0:T(8,128)(2,1)}) custom-call(s32[16]{0:T(128)} %lags_ref.1, s32[2048]{0:T(1024)} %bitcast.128, s32[1]{0:T(128)} %bitcast.1.mine_ref, bf16[16,2,8,1024]{3,2,1,0:T(8,128)(2,1)} %bitcast.121, bf16[2,3,2048,128]{3,2,1,0:T(8,128)(2,1)} %weights_ref.1), custom_call_target="tpu_custom_call" | custom-call | tf_op jit(solution)/shard_map/bands/pallas_call | solution.py:124
  45.0 0.1 collective-permute-start
  45.1 2.7 %collective-permute-done = bf16[8,128,512]{2,1,0:T(8,128)(2,1)S(1)} collective-permute-done((bf16[8,128,512]{2,1,0:T(8,128)(2,1)}, bf16[8,128,512]{2,1,0:T(8,128)(2,1)S(1)}, u32[]{:S(2)}, u32[]{:S(2)}) %collective-permute-start) | collective-permute-done | bytes 1048608 | tf_op jit(solution)/shard_map/ppermute | solution.py:169
  47.8 2.0 %convert_add_fusion = f32[8,128,512]{2,1,0:T(8,128)S(1)} fusion(f32[8,128,512]{2,1,0:T(8,128)} %get-tuple-element.7, bf16[8,128,512]{2,1,0:T(8,128)(2,1)S(1)} %collective-permute-done), kind=kLoop, calls=%fused_computation | loop fusion | flops 1048576 | bytes 5242880 | tf_op jit(solution)/shard_map/add | solution.py:169
  49.8 0.1 split.21
  49.9 0.8 fusion
  50.6 1.0 %collective-permute-start.1 = (bf16[4,64,512]{2,1,0:T(8,128)(2,1)}, bf16[4,64,512]{2,1,0:T(8,128)(2,1)S(1)}, u32[]{:S(2)}, u32[]{:S(2)}) collective-permute-start(bf16[4,64,512]{2,1,0:T(8,128)(2,1)} %fusion), channel_id=1, source_target_pairs={{0,4},{2,6},{4,0},{6,2},{8,12},{10,14},{12,8},{14,10},{16,20},{18,... | collective-permute-start | bytes 786440 | tf_op jit(solution)/shard_map/ppermute | solution.py:160
  51.7 1.6 %collective-permute-start.5 = (bf16[8,64,256]{2,1,0:T(8,128)(2,1)S(1)}, bf16[8,64,256]{2,1,0:T(8,128)(2,1)S(1)}, u32[]{:S(2)}, u32[]{:S(2)}) collective-permute-start(bf16[8,64,256]{2,1,0:T(8,128)(2,1)S(1)} %select_convert_fusion), channel_id=1, source_target_pairs={{0,1},{1,0},{2,3},{3,2},{4,5},{5,4},{6,7},{7,6},{8,9},{9,8},{10,11... | collective-permute-start | bytes 786440 | tf_op jit(solution)/shard_map/ppermute | solution.py:160
  53.3 5.9 %collective-permute-done.1 = bf16[4,64,512]{2,1,0:T(8,128)(2,1)S(1)} collective-permute-done((bf16[4,64,512]{2,1,0:T(8,128)(2,1)}, bf16[4,64,512]{2,1,0:T(8,128)(2,1)S(1)}, u32[]{:S(2)}, u32[]{:S(2)}) %collective-permute-start.1) | collective-permute-done | bytes 262176 | tf_op jit(solution)/shard_map/ppermute | solution.py:160
  59.2 0.1 bitcast_add_fusion
  59.4 1.6 %collective-permute-start.2 = (bf16[4,64,256]{2,1,0:T(8,128)(2,1)S(1)}, bf16[4,64,256]{2,1,0:T(8,128)(2,1)S(1)}, u32[]{:S(2)}, u32[]{:S(2)}) collective-permute-start(bf16[4,64,256]{2,1,0:T(8,128)(2,1)S(1)} %select_convert_fusion.3), channel_id=1, source_target_pairs={{0,1},{1,0},{2,3},{3,2},{4,5},{5,4},{6,7},{7,6},{8,9},{9,8},{10,11... | collective-permute-start | bytes 393224 | tf_op jit(solution)/shard_map/ppermute | solution.py:160
  61.0 0.0 collective-permute-done.5
  61.0 0.1 convert_add_fusion.1
  61.1 1.3 %collective-permute-start.6 = (bf16[4,64,256]{2,1,0:T(8,128)(2,1)S(1)}, bf16[4,64,256]{2,1,0:T(8,128)(2,1)S(1)}, u32[]{:S(2)}, u32[]{:S(2)}) collective-permute-start(bf16[4,64,256]{2,1,0:T(8,128)(2,1)S(1)} %fusion.1), channel_id=1, source_target_pairs={{0,4},{2,6},{4,0},{6,2},{8,12},{10,14},{12,8},{14,10},{16,20},{18,... | collective-permute-start | bytes 393224 | tf_op jit(solution)/shard_map/ppermute | solution.py:160
  62.4 2.0 %collective-permute-done.2 = bf16[4,64,256]{2,1,0:T(8,128)(2,1)S(1)} collective-permute-done((bf16[4,64,256]{2,1,0:T(8,128)(2,1)S(1)}, bf16[4,64,256]{2,1,0:T(8,128)(2,1)S(1)}, u32[]{:S(2)}, u32[]{:S(2)}) %collective-permute-start.2) | collective-permute-done | bytes 131104 | tf_op jit(solution)/shard_map/ppermute | solution.py:160
  64.5 1.8 %collective-permute-start.3 = (bf16[2,64,256]{2,1,0:T(8,128)(2,1)S(1)}, bf16[2,64,256]{2,1,0:T(8,128)(2,1)S(1)}, u32[]{:S(2)}, u32[]{:S(2)}) collective-permute-start(bf16[2,64,256]{2,1,0:T(8,128)(2,1)S(1)} %fusion.6), channel_id=1, source_target_pairs={{0,8},{2,10},{4,12},{6,14},{8,0},{10,2},{12,4},{14,6},{16,24},{18,... | collective-permute-start | bytes 196616 | tf_op jit(solution)/shard_map/ppermute | solution.py:160
  66.3 0.0 collective-permute-done.6
  66.4 1.6 %collective-permute-start.7 = (bf16[2,64,256]{2,1,0:T(8,128)(2,1)S(1)}, bf16[2,64,256]{2,1,0:T(8,128)(2,1)S(1)}, u32[]{:S(2)}, u32[]{:S(2)}) collective-permute-start(bf16[2,64,256]{2,1,0:T(8,128)(2,1)S(1)} %fusion.7), channel_id=1, source_target_pairs={{0,8},{2,10},{4,12},{6,14},{8,0},{10,2},{12,4},{14,6},{16,24},{18,... | collective-permute-start | bytes 196616 | tf_op jit(solution)/shard_map/ppermute | solution.py:160
  68.0 0.8 %collective-permute-done.3 = bf16[2,64,256]{2,1,0:T(8,128)(2,1)S(1)} collective-permute-done((bf16[2,64,256]{2,1,0:T(8,128)(2,1)S(1)}, bf16[2,64,256]{2,1,0:T(8,128)(2,1)S(1)}, u32[]{:S(2)}, u32[]{:S(2)}) %collective-permute-start.3) | collective-permute-done | bytes 65568 | tf_op jit(solution)/shard_map/ppermute | solution.py:160
  68.9 2.5 %collective-permute-start.4 = (bf16[1,64,256]{2,1,0:T(8,128)(2,1)S(1)}, bf16[1,64,256]{2,1,0:T(8,128)(2,1)S(1)}, u32[]{:S(2)}, u32[]{:S(2)}) collective-permute-start(bf16[1,64,256]{2,1,0:T(8,128)(2,1)S(1)} %fusion.10), channel_id=1, source_target_pairs={{0,16},{2,18},{4,20},{6,22},{8,24},{10,26},{12,28},{14,30},{16,0},... | collective-permute-start | bytes 98312 | tf_op jit(solution)/shard_map/ppermute | solution.py:160
  71.3 0.0 collective-permute-done.7
  71.4 1.7 %collective-permute-start.8 = (bf16[1,64,256]{2,1,0:T(8,128)(2,1)S(1)}, bf16[1,64,256]{2,1,0:T(8,128)(2,1)S(1)}, u32[]{:S(2)}, u32[]{:S(2)}) collective-permute-start(bf16[1,64,256]{2,1,0:T(8,128)(2,1)S(1)} %fusion.11), channel_id=1, source_target_pairs={{0,16},{2,18},{4,20},{6,22},{8,24},{10,26},{12,28},{14,30},{16,0},... | collective-permute-start | bytes 98312 | tf_op jit(solution)/shard_map/ppermute | solution.py:160
  73.1 0.7 collective-permute-done.4
  73.7 2.5 %collective-permute-done.8 = bf16[1,64,256]{2,1,0:T(8,128)(2,1)S(1)} collective-permute-done((bf16[1,64,256]{2,1,0:T(8,128)(2,1)S(1)}, bf16[1,64,256]{2,1,0:T(8,128)(2,1)S(1)}, u32[]{:S(2)}, u32[]{:S(2)}) %collective-permute-start.8) | collective-permute-done | bytes 32800 | tf_op jit(solution)/shard_map/ppermute | solution.py:160
  76.3 0.7 pad_maximum_fusion
  (14 shorter events, 0.3 us)
Async XLA Ops:
  5.7 21.7 %all-to-all-start = ((bf16[16,16,1024]{2,1,0:T(8,128)(2,1)}), bf16[16,16,1024]{2,1,0:T(8,128)(2,1)S(1)}, u32[]{:S(2)}, u32[]{:S(2)}) async-start(bf16[16,16,1024]{2,1,0:T(8,128)(2,1)} %bitcast.122), calls=%async_computation | async-start | bytes 1048576 | tf_op jit(solution)/shard_map/all_to_all | solution.py:181
  27.4 0.8 %copy-start = (bf16[16,16,1024]{2,1,0:T(8,128)(2,1)}, bf16[16,16,1024]{2,1,0:T(8,128)(2,1)S(1)}, u32[]{:S(2)}) copy-start(bf16[16,16,1024]{2,1,0:T(8,128)(2,1)S(1)} %all-to-all-done) | copy-start | bytes 1572868
  45.0 2.9 %collective-permute-start = (bf16[8,128,512]{2,1,0:T(8,128)(2,1)}, bf16[8,128,512]{2,1,0:T(8,128)(2,1)S(1)}, u32[]{:S(2)}, u32[]{:S(2)}) collective-permute-start(bf16[8,128,512]{2,1,0:T(8,128)(2,1)} %get-tuple-element.8), channel_id=1, source_target_pairs={{0,2},{2,0},{4,6},{6,4},{8,10},{10,8},{12,14},{14,12},{16,18},{18,... | collective-permute-start | bytes 3145736 | tf_op jit(solution)/shard_map/ppermute | solution.py:169
  50.6 8.6 %collective-permute-start.1 = (bf16[4,64,512]{2,1,0:T(8,128)(2,1)}, bf16[4,64,512]{2,1,0:T(8,128)(2,1)S(1)}, u32[]{:S(2)}, u32[]{:S(2)}) collective-permute-start(bf16[4,64,512]{2,1,0:T(8,128)(2,1)} %fusion), channel_id=1, source_target_pairs={{0,4},{2,6},{4,0},{6,2},{8,12},{10,14},{12,8},{14,10},{16,20},{18,... | collective-permute-start | bytes 786440 | tf_op jit(solution)/shard_map/ppermute | solution.py:160
  51.7 9.2 %collective-permute-start.5 = (bf16[8,64,256]{2,1,0:T(8,128)(2,1)S(1)}, bf16[8,64,256]{2,1,0:T(8,128)(2,1)S(1)}, u32[]{:S(2)}, u32[]{:S(2)}) collective-permute-start(bf16[8,64,256]{2,1,0:T(8,128)(2,1)S(1)} %select_convert_fusion), channel_id=1, source_target_pairs={{0,1},{1,0},{2,3},{3,2},{4,5},{5,4},{6,7},{7,6},{8,9},{9,8},{10,11... | collective-permute-start | bytes 786440 | tf_op jit(solution)/shard_map/ppermute | solution.py:160
  59.4 5.0 %collective-permute-start.2 = (bf16[4,64,256]{2,1,0:T(8,128)(2,1)S(1)}, bf16[4,64,256]{2,1,0:T(8,128)(2,1)S(1)}, u32[]{:S(2)}, u32[]{:S(2)}) collective-permute-start(bf16[4,64,256]{2,1,0:T(8,128)(2,1)S(1)} %select_convert_fusion.3), channel_id=1, source_target_pairs={{0,1},{1,0},{2,3},{3,2},{4,5},{5,4},{6,7},{7,6},{8,9},{9,8},{10,11... | collective-permute-start | bytes 393224 | tf_op jit(solution)/shard_map/ppermute | solution.py:160
  61.1 5.2 %collective-permute-start.6 = (bf16[4,64,256]{2,1,0:T(8,128)(2,1)S(1)}, bf16[4,64,256]{2,1,0:T(8,128)(2,1)S(1)}, u32[]{:S(2)}, u32[]{:S(2)}) collective-permute-start(bf16[4,64,256]{2,1,0:T(8,128)(2,1)S(1)} %fusion.1), channel_id=1, source_target_pairs={{0,4},{2,6},{4,0},{6,2},{8,12},{10,14},{12,8},{14,10},{16,20},{18,... | collective-permute-start | bytes 393224 | tf_op jit(solution)/shard_map/ppermute | solution.py:160
  64.5 4.3 %collective-permute-start.3 = (bf16[2,64,256]{2,1,0:T(8,128)(2,1)S(1)}, bf16[2,64,256]{2,1,0:T(8,128)(2,1)S(1)}, u32[]{:S(2)}, u32[]{:S(2)}) collective-permute-start(bf16[2,64,256]{2,1,0:T(8,128)(2,1)S(1)} %fusion.6), channel_id=1, source_target_pairs={{0,8},{2,10},{4,12},{6,14},{8,0},{10,2},{12,4},{14,6},{16,24},{18,... | collective-permute-start | bytes 196616 | tf_op jit(solution)/shard_map/ppermute | solution.py:160
  66.4 5.0 %collective-permute-start.7 = (bf16[2,64,256]{2,1,0:T(8,128)(2,1)S(1)}, bf16[2,64,256]{2,1,0:T(8,128)(2,1)S(1)}, u32[]{:S(2)}, u32[]{:S(2)}) collective-permute-start(bf16[2,64,256]{2,1,0:T(8,128)(2,1)S(1)} %fusion.7), channel_id=1, source_target_pairs={{0,8},{2,10},{4,12},{6,14},{8,0},{10,2},{12,4},{14,6},{16,24},{18,... | collective-permute-start | bytes 196616 | tf_op jit(solution)/shard_map/ppermute | solution.py:160
  68.9 4.9 %collective-permute-start.4 = (bf16[1,64,256]{2,1,0:T(8,128)(2,1)S(1)}, bf16[1,64,256]{2,1,0:T(8,128)(2,1)S(1)}, u32[]{:S(2)}, u32[]{:S(2)}) collective-permute-start(bf16[1,64,256]{2,1,0:T(8,128)(2,1)S(1)} %fusion.10), channel_id=1, source_target_pairs={{0,16},{2,18},{4,20},{6,22},{8,24},{10,26},{12,28},{14,30},{16,0},... | collective-permute-start | bytes 98312 | tf_op jit(solution)/shard_map/ppermute | solution.py:160
  71.4 4.9 %collective-permute-start.8 = (bf16[1,64,256]{2,1,0:T(8,128)(2,1)S(1)}, bf16[1,64,256]{2,1,0:T(8,128)(2,1)S(1)}, u32[]{:S(2)}, u32[]{:S(2)}) collective-permute-start(bf16[1,64,256]{2,1,0:T(8,128)(2,1)S(1)} %fusion.11), channel_id=1, source_target_pairs={{0,16},{2,18},{4,20},{6,22},{8,24},{10,26},{12,28},{14,30},{16,0},... | collective-permute-start | bytes 98312 | tf_op jit(solution)/shard_map/ppermute | solution.py:160
where the time goes:
time: 77.5 us; the launch traced here: 76.9 us
  waiting for transfers between devices  28.9 us (37%)
  starting transfers between devices  20.7 us (27%)
  Pallas kernels  19.5 us (25%)
  other arithmetic  4.73 us (6%)
  local copies, waits for them, and re-layouts  3.06 us (4%)
    pallas_call x1, Pallas kernels, banded_call(): pl.pallas_call(kernel, out_shape=outs, grid_spec=pltpu.PrefetchScalarGrid...  16.7 us
    all_to_all x1, waiting for transfers between devices, local(): lax.all_to_all(outgoing, 'cfd', split_axis=0, concat_axis=0, tiled=True)  14.3 us
    ppermute x8, starting transfers between devices, halve(): return kept + lax.ppermute(sent, axis, partners).astype(jnp.float32)  13.2 us
    ppermute x8, waiting for transfers between devices, halve(): return kept + lax.ppermute(sent, axis, partners).astype(jnp.float32)  11.9 us
    all_to_all x1, starting transfers between devices, local(): lax.all_to_all(outgoing, 'cfd', split_axis=0, concat_axis=0, tiled=True)  7.39 us
    pallas_call x1, Pallas kernels, prepare(): pl.pallas_call(prepare_kernel, out_shape=jax.ShapeDtypeStruct((2 * faces,...  2.74 us
    ppermute x1, waiting for transfers between devices, exchange_sums(): total = kept + lax.ppermute(sent, 'cfd', partners).astype(jnp.float32)  2.74 us
    add x1, other arithmetic, exchange_sums(): total = kept + lax.ppermute(sent, 'cfd', partners).astype(jnp.float32)  1.98 us
  transfers between devices with their start and end apart: 10, of which 7 were waited for; matrix products, arithmetic and copies ran while one was open for 1% of the time, Pallas kernels for 0%

commit v1 on v0

--- a/solution.py
+++ b/solution.py
@@ -173,7 +173,380 @@
     return jnp.concatenate([part[0] for part in streams], axis=0)
 
 
-def local(surface_raw, area_normals, kernel_weights, block_map, band_observers, band_lags):
+def flip(place, mask):
+    out = place
+    for bit in range(mask.bit_length()):
+        if mask >> bit & 1:
+            out = out + (1 << bit) * (1 - 2 * lax.rem(lax.div(place, 1 << bit), 2))
+    return out
+
+
+def fused_kernel(
+    lags_ref,
+    map_ref,
+    ids_ref,
+    normals_ref,
+    surface_ref,
+    weights_ref,
+    out_ref,
+    surface,
+    weights,
+    normals,
+    outgoing,
+    arrived,
+    sources,
+    spread,
+    found,
+    inverse,
+    slots,
+    rows,
+    core_out,
+    core_in,
+    x_out,
+    x_in,
+    x_kept,
+    y_out,
+    y_in,
+    y_kept,
+    xy_out,
+    xy_in,
+    z_out,
+    z_in,
+    load_sems,
+    block_send,
+    block_recv,
+    core_send,
+    core_recv,
+    first_send,
+    first_recv,
+    second_send,
+    second_recv,
+    z_send,
+    z_recv,
+):
+    me = lax.axis_index("cfd")
+    owners = outgoing.shape[0]
+    zs = owners // 4
+    core, x, z = lax.rem(me, 2), lax.rem(lax.div(me, 2), 2), lax.div(me, 4)
+    y = lax.axis_index("ac")
+    taps, terms, observers, faces = weights.shape
+    bands, width = ids_ref.shape
+    size, steps = surface.shape[2:]
+    out_len = steps // 2
+    chunks = out_len // LANES
+    height = observers // owners
+    near = owners // zs
+
+    get_surface = pltpu.make_async_copy(surface_ref, surface, load_sems.at[0])
+    get_weights = pltpu.make_async_copy(weights_ref, weights, load_sems.at[1])
+    get_surface.start()
+
+    def remote(src, dst, send, recv, **peer):
+        return pltpu.make_async_remote_copy(
+            src_ref=src, dst_ref=dst, send_sem=send, recv_sem=recv,
+            device_id=peer, device_id_type=pl.DeviceIdType.MESH,
+        )
+
+    barrier = pltpu.get_barrier_semaphore()
+    for k in range(1, owners):
+        pl.semaphore_signal(
+            barrier, inc=1, device_id={"cfd": flip(me, k)}, device_id_type=pl.DeviceIdType.MESH
+        )
+    pl.semaphore_signal(barrier, inc=1, device_id={"ac": 1 - y}, device_id_type=pl.DeviceIdType.MESH)
+
+    wide = normals_ref[...].astype(jnp.float32)
+    tall = jnp.concatenate([wide, jnp.zeros((LANES - wide.shape[0], faces), jnp.float32)], axis=0)
+    normals[...] = tall.T.reshape(owners, size, LANES)
+    get_surface.wait()
+    get_weights.start()
+    pl.semaphore_wait(barrier, owners)
+
+    def thick_block(place):
+        along = surface[2, place].astype(jnp.float32) * normals[place, :, 0:1]
+        along = along + surface[3, place].astype(jnp.float32) * normals[place, :, 1:2]
+        along = along + surface[4, place].astype(jnp.float32) * normals[place, :, 2:3]
+        return (surface[1, place].astype(jnp.float32) * along).astype(jnp.bfloat16)
+
+    block_copies = {}
+    order = sorted(range(1, owners), key=lambda k: SEND_ORDER(k, near))
+    for k in order:
+        peer = flip(me, k)
+        place = map_ref[peer]
+        outgoing[k, 0] = thick_block(place)
+        outgoing[k, 1] = surface[0, place]
+        block_copies[k] = remote(
+            outgoing.at[k], arrived.at[me], block_send.at[k], block_recv.at[k], cfd=peer
+        )
+        block_copies[k].start()
+    place = map_ref[me]
+    arrived[me, 0] = thick_block(place)
+    arrived[me, 1] = surface[0, place]
+
+    ids = ids_ref[...]
+    down = jnp.concatenate([ids, jnp.zeros((LANES - bands, width), jnp.int32)], axis=0).T
+    for b in range(bands):
+        spread[b] = jnp.broadcast_to(down[:, b : b + 1], (width, LANES))
+    lane = lax.broadcasted_iota(jnp.int32, (width, LANES), 1)
+    slot = lax.broadcasted_iota(jnp.int32, (width, LANES), 0)
+
+    @pl.loop(0, observers // LANES)
+    def _(part):
+        def add(b, total):
+            hit = spread[b] == lane + part * LANES
+            return jnp.where(hit, slot + b * width, total)
+
+        total = lax.fori_loop(0, bands, add, jnp.zeros((width, LANES), jnp.int32))
+        found[pl.ds(part, 1), :] = jnp.max(total, axis=0, keepdims=True)
+
+    get_inverse = pltpu.make_async_copy(found, inverse, load_sems.at[2])
+    get_inverse.start()
+
+    step = lax.broadcasted_iota(jnp.int32, (near * size, steps), 1)
+
+    def rate(series):
+        moved = jnp.where(step > 0, series - pltpu.roll(series, 1, 1), 0.0)
+        return moved.astype(jnp.bfloat16).astype(jnp.float32)
+
+    for j in [0, 1] + list(range(2, zs)):
+        for k in range(near * j, near * j + near):
+            if k:
+                block_copies[k].wait()
+        first = flip(z, j) * near
+        series = arrived[pl.ds(first, near)].astype(jnp.float32)
+        thick = series[:, 0].reshape(near * size, steps)
+        pressure = series[:, 1].reshape(near * size, steps)
+        for c, value in enumerate((rate(thick), rate(pressure), pressure)):
+            for k in range(taps):
+                late = pltpu.roll(value, k, 1) if k else value
+                top = (k * terms + c) * faces + first * size
+                here = pl.ds(pl.multiple_of(top, near * size), near * size)
+                for t in range(steps // LANES):
+                    sources[t, here, :] = late[:, t * LANES : (t + 1) * LANES].astype(jnp.bfloat16)
+    get_weights.wait()
+
+    @pl.loop(0, bands)
+    def _(b):
+        start = out_len - lags_ref[b]
+        tile = jnp.minimum(lax.div(start, LANES), steps // LANES - chunks - 1)
+        rest = start - tile * LANES
+        shift = lax.rem(LANES - rest, LANES)
+        here = pl.ds(pl.multiple_of(b * width, width), width)
+        chosen = jnp.concatenate(
+            [weights[k, c, here, :] for k in range(taps) for c in range(terms)], axis=1
+        )
+        window = jnp.concatenate([sources[tile + t] for t in range(chunks + 1)], axis=1)
+        whole = jnp.dot(chosen, window, preferred_element_type=jnp.float32)
+        parts = [
+            pltpu.roll(whole[:, t * LANES : (t + 1) * LANES], shift, 1) for t in range(chunks + 1)
+        ]
+        for t in range(chunks):
+            slots[pl.ds(b * (width * chunks) + t, width, stride=chunks), :] = jnp.where(
+                lane < LANES - rest, parts[t], parts[t + 1]
+            )
+
+    get_inverse.wait()
+    unroll = 32
+
+    def gather(owner):
+        base = owner * height
+
+        @pl.loop(0, height // unroll)
+        def _(group):
+            for m in range(unroll):
+                at = base + group * unroll + m
+                found_at = inverse[lax.div(at, LANES), lax.rem(at, LANES)]
+                value = slots.reshape(observers, chunks, LANES)[found_at]
+                rows[pl.ds(pl.multiple_of(at * chunks, chunks), chunks), :] = value
+
+    def unit(owner, t):
+        return rows[pl.ds(owner * (height * chunks) + t, height, stride=chunks), :]
+
+    def narrow(value):
+        return value.astype(jnp.bfloat16)
+
+    def wide_of(value):
+        return value.astype(jnp.float32)
+
+    half = chunks // 2
+    core_copies, x_copies, y_copies, xy_copies, yx_copies, z_copies = {}, {}, {}, {}, {}, {}
+    turn = list(range(2, zs)) + [1, 0]
+
+    def send_core(j):
+        top = flip(z, j) * near
+        for other in range(2):
+            gather(top + other * 2 + 1 - core)
+        for other in range(2):
+            for t in range(chunks):
+                core_out[j, other, t] = narrow(unit(top + other * 2 + 1 - core, t))
+        core_copies[j] = remote(
+            core_out.at[j], core_in.at[j], core_send.at[j], core_recv.at[j], cfd=flip(me, 1)
+        )
+        core_copies[j].start()
+        for other in range(2):
+            gather(top + other * 2 + core)
+
+    def send_first(j):
+        top = flip(z, j) * near
+        core_copies[j].wait()
+
+        def total(other, t):
+            return unit(top + other * 2 + core, t) + wide_of(core_in[j, other, t])
+
+        for side in range(2):
+            x_out[j, side] = narrow(total(1 - x, side * half))
+        x_copies[j] = remote(
+            x_out.at[j], x_in.at[j], first_send.at[0, j], first_recv.at[0, j], cfd=flip(me, 2)
+        )
+        x_copies[j].start()
+        for other in range(2):
+            y_out[j, other] = narrow(total(other, (1 - y) * half + 1))
+        y_copies[j] = remote(
+            y_out.at[j], y_in.at[j], first_send.at[1, j], first_recv.at[1, j], ac=1 - y
+        )
+        y_copies[j].start()
+        for side in range(2):
+            x_kept[j, side] = total(x, side * half)
+        for other in range(2):
+            y_kept[j, other] = total(other, y * half + 1)
+
+    def send_second(j):
+        x_copies[j].wait()
+        xy_out[0, j] = narrow(x_kept[j, 1 - y] + wide_of(x_in[j, 1 - y]))
+        xy_copies[j] = remote(
+            xy_out.at[0, j], xy_in.at[0, j], second_send.at[0, j], second_recv.at[0, j], ac=1 - y
+        )
+        xy_copies[j].start()
+        y_copies[j].wait()
+        xy_out[1, j] = narrow(y_kept[j, 1 - x] + wide_of(y_in[j, 1 - x]))
+        yx_copies[j] = remote(
+            xy_out.at[1, j], xy_in.at[1, j], second_send.at[1, j], second_recv.at[1, j],
+            cfd=flip(me, 2),
+        )
+        yx_copies[j].start()
+
+    def finish_second(j):
+        xy_copies[j].wait()
+        from_x = x_kept[j, y] + wide_of(x_in[j, y]) + wide_of(xy_in[0, j])
+        yx_copies[j].wait()
+        from_y = y_kept[j, x] + wide_of(y_in[j, x]) + wide_of(xy_in[1, j])
+        return from_x, from_y
+
+    def send_z(j):
+        for stream, value in enumerate(finish_second(j)):
+            z_out[j, stream] = narrow(value)
+        z_copies[j] = remote(
+            z_out.at[j], z_in.at[j], z_send.at[j], z_recv.at[j], cfd=flip(me, near * j)
+        )
+        z_copies[j].start()
+
+    for place, j in enumerate(turn):
+        send_core(j)
+        if place:
+            send_first(turn[place - 1])
+    send_first(turn[-1])
+    for j in turn:
+        send_second(j)
+    for j in turn[:-1]:
+        send_z(j)
+    results = list(finish_second(0))
+    for j in turn[:-1]:
+        z_copies[j].wait()
+        results = [value + wide_of(z_in[j, s]) for s, value in enumerate(results)]
+    for s, value in enumerate(results):
+        out_ref[:, s * LANES : (s + 1) * LANES] = value
+
+
+def SEND_ORDER(k, near):
+    j = k // near
+    return (0, 3, 1, 2)[j] if j < 4 else j, k
+
+
+def fused(surface_raw, area_normals, kernel_weights, block_map, band_observers, band_lags):
+    owners, halves = lax.axis_size("cfd"), lax.axis_size("ac")
+    faces, steps = surface_raw.shape[1:]
+    taps, terms, observers, _ = kernel_weights.shape
+    bands, width = band_observers.shape
+    size, height = faces // owners, observers // owners
+    chunks = steps // 2 // LANES
+    zs = owners // 4
+    near = owners // zs
+    bf16, f32, i32 = jnp.bfloat16, jnp.float32, jnp.int32
+    tile = (height, LANES)
+    dma = pltpu.SemaphoreType.DMA
+    vmem, smem, hbm = (
+        pl.BlockSpec(memory_space=space) for space in (pltpu.VMEM, pltpu.SMEM, pl.ANY)
+    )
+    return pl.pallas_call(
+        fused_kernel,
+        out_shape=jax.ShapeDtypeStruct((height, chunks // halves * LANES), f32),
+        in_specs=[smem, smem, vmem, vmem, hbm, hbm],
+        out_specs=vmem,
+        scratch_shapes=[
+            pltpu.VMEM((surface_raw.shape[0], owners, size, steps), bf16),
+            pltpu.VMEM(kernel_weights.shape, bf16),
+            pltpu.VMEM((owners, size, LANES), f32),
+            pltpu.VMEM((owners, 2, size, steps), bf16),
+            pltpu.VMEM((owners, 2, size, steps), bf16),
+            pltpu.VMEM((steps // LANES, taps * terms * faces, LANES), bf16),
+            pltpu.VMEM((bands, width, LANES), i32),
+            pltpu.VMEM((observers // LANES, LANES), i32),
+            pltpu.SMEM((observers // LANES, LANES), i32),
+            pltpu.VMEM((observers * chunks, LANES), f32),
+            pltpu.VMEM((observers * chunks, LANES), f32),
+            pltpu.VMEM((zs, 2, chunks) + tile, bf16),
+            pltpu.VMEM((zs, 2, chunks) + tile, bf16),
+            pltpu.VMEM((zs, 2) + tile, bf16),
+            pltpu.VMEM((zs, 2) + tile, bf16),
+            pltpu.VMEM((zs, 2) + tile, f32),
+            pltpu.VMEM((zs, 2) + tile, bf16),
+            pltpu.VMEM((zs, 2) + tile, bf16),
+            pltpu.VMEM((zs, 2) + tile, f32),
+            pltpu.VMEM((2, zs) + tile, bf16),
+            pltpu.VMEM((2, zs) + tile, bf16),
+            pltpu.VMEM((zs, 2) + tile, bf16),
+            pltpu.VMEM((zs, 2) + tile, bf16),
+            dma((3,)),
+            dma((owners,)),
+            dma((owners,)),
+            dma((zs,)),
+            dma((zs,)),
+            dma((2, zs)),
+            dma((2, zs)),
+            dma((2, zs)),
+            dma((2, zs)),
+            dma((zs,)),
+            dma((zs,)),
+        ],
+        compiler_params=pltpu.CompilerParams(
+            collective_id=0, has_side_effects=True, vmem_limit_bytes=60 * 2**20
+        ),
+        name="fused",
+    )(
+        band_lags,
+        block_map[0, 0],
+        band_observers,
+        area_normals,
+        surface_raw.reshape(surface_raw.shape[0], owners, size, steps),
+        kernel_weights,
+    )
+
+
+def fits_fused(owners, halves, surface_raw, kernel_weights, band_observers):
+    faces, steps = surface_raw.shape[1:]
+    tiles = halves * 2
+    return (
+        halves == 2
+        and owners % 4 == 0
+        and owners & (owners - 1) == 0
+        and faces == LANES
+        and band_observers.shape[1] == LANES
+        and faces // owners % 8 == 0
+        and steps == 2 * tiles * LANES
+        and kernel_weights.shape[2] % (owners * 32) == 0
+    )
+
+
+def general(surface_raw, area_normals, kernel_weights, block_map, band_observers, band_lags):
     blocks = lax.axis_size("cfd")
     faces, steps = surface_raw.shape[1:]
     size = faces // blocks
@@ -195,6 +568,13 @@
     return exchange_sums(kept, sent)
 
 
+def local(surface_raw, area_normals, kernel_weights, block_map, band_observers, band_lags):
+    owners, halves = lax.axis_size("cfd"), lax.axis_size("ac")
+    fast = fits_fused(owners, halves, surface_raw, kernel_weights, band_observers)
+    run = fused if fast else general
+    return run(surface_raw, area_normals, kernel_weights, block_map, band_observers, band_lags)
+
+
 def solution(mesh):
     placed = (
         P(None, ("cfd", "ac"), None),

time: 77.5 us -> 52.2 us (0.67)
  Pallas kernels: 19.5 us -> 50.4 us
  waiting for transfers between devices: 28.9 us -> 0 us
  starting transfers between devices: 20.7 us -> 0 us
  other arithmetic: 4.73 us -> 0 us
  local copies, waits for them, and re-layouts: 3.06 us -> 1.57 us
    pallas_call x2 -> x1, Pallas kernels: 19.5 us -> 50.4 us  [fused(): pl.pallas_call(fused_kernel, out_shape=jax.ShapeDtypeStruct((height, chun...]
    ppermute x9 -> x0, waiting for transfers between devices: 14.6 us -> none  [the longest x8 11.9 us: halve(): return kept + lax.ppermute(sent, axis, partners).astype(jnp.float32)]
    all_to_all x1 -> x0, waiting for transfers between devices: 14.3 us -> none  [local(): lax.all_to_all(outgoing, 'cfd', split_axis=0, concat_axis=0, tiled=True)]
    ppermute x9 -> x0, starting transfers between devices: 13.3 us -> none  [the longest x8 13.2 us: halve(): return kept + lax.ppermute(sent, axis, partners).astype(jnp.float32)]
    all_to_all x1 -> x0, starting transfers between devices: 7.39 us -> none  [local(): lax.all_to_all(outgoing, 'cfd', split_axis=0, concat_axis=0, tiled=True)]
    add x7 -> x0, other arithmetic: 2.43 us -> none  [the longest x1 1.98 us: exchange_sums(): total = kept + lax.ppermute(sent, 'cfd', partners).astype(jnp.float32)]
    convert_element_type x1 -> x0, local copies, waits for them, and re-layouts: 1.41 us -> none  [prepare(): area_normals.T.astype(jnp.float32)]
    convert_element_type x8 -> x0, other arithmetic: 0.91 us -> none  [halve(): sent = jnp.where(mine == 1, first, second).astype(jnp.bfloat16)]
  transfers between devices with their start and end apart: 10 -> 0, of which waited for: 7 -> 0; matrix products, arithmetic and copies ran while one was open for 1% -> 0% of each run, Pallas kernels for 0% -> 0%
where the time goes in v1:
time: 52.2 us; the launch traced here: 52 us
  Pallas kernels  50.4 us (97%)
  local copies, waits for them, and re-layouts  1.57 us (3%)
    pallas_call x1, Pallas kernels, fused(): pl.pallas_call(fused_kernel, out_shape=jax.ShapeDtypeStruct((height, chun...  50.4 us
    unnamed x1, local copies, waits for them, and re-layouts  1.57 us

profile of v1, /device:TPU:0, one launch (start us, length us, event | category | flops | bytes accessed | tf_op | source)
XLA Modules:
  0.0 52.0 jit_solution(4953543611826468258)
XLA Ops:
  0.0 50.4 %fused.1 = f32[128,256]{1,0:T(8,128)} custom-call(s32[16]{0:T(128)} %lags_ref.1, s32[16]{0:T(128)} %bitcast.3, s32[16,128]{1,0:T(8,128)} %ids_ref.1, bf16[3,128]{1,0:T(4,128)(2,1)} %normals_ref.1, bf16[5,16,8,1024]{3,2,1,0:T(8,128)(2,1)} %bitcast.2, bf16[2,3,2048,128]{3,2,1,0:T(8,128)(2,1)} %weights_ref.1), custom_call_target="tpu_custom_call" | custom-call | tf_op jit(solution)/shard_map/fused/pallas_call | solution.py:479
  50.4 1.6 %copy.8 = f32[128,256]{1,0:T(8,128)} copy(f32[128,256]{1,0:T(8,128)} %fused.1) | data formatting | bytes 262144

commit v2 on v1

--- a/solution.py
+++ b/solution.py
@@ -188,13 +188,16 @@
     normals_ref,
     surface_ref,
     weights_ref,
-    out_ref,
+    first_ref,
+    second_ref,
     surface,
     weights,
     normals,
     outgoing,
     arrived,
     sources,
+    before,
+    wide,
     spread,
     found,
     inverse,
@@ -225,7 +228,8 @@
     z_recv,
 ):
     me = lax.axis_index("cfd")
-    owners = outgoing.shape[0]
+    owners, pieces = outgoing.shape[:2]
+    span = outgoing.shape[-1]
     zs = owners // 4
     core, x, z = lax.rem(me, 2), lax.rem(lax.div(me, 2), 2), lax.div(me, 4)
     y = lax.axis_index("ac")
@@ -254,12 +258,11 @@
         )
     pl.semaphore_signal(barrier, inc=1, device_id={"ac": 1 - y}, device_id_type=pl.DeviceIdType.MESH)
 
-    wide = normals_ref[...].astype(jnp.float32)
-    tall = jnp.concatenate([wide, jnp.zeros((LANES - wide.shape[0], faces), jnp.float32)], axis=0)
+    flat = normals_ref[...].astype(jnp.float32)
+    tall = jnp.concatenate([flat, jnp.zeros((LANES - flat.shape[0], faces), jnp.float32)], axis=0)
     normals[...] = tall.T.reshape(owners, size, LANES)
     get_surface.wait()
     get_weights.start()
-    pl.semaphore_wait(barrier, owners)
 
     def thick_block(place):
         along = surface[2, place].astype(jnp.float32) * normals[place, :, 0:1]
@@ -267,20 +270,31 @@
         along = along + surface[4, place].astype(jnp.float32) * normals[place, :, 2:3]
         return (surface[1, place].astype(jnp.float32) * along).astype(jnp.bfloat16)
 
+    def cut(value, c):
+        return value[:, c * span : (c + 1) * span]
+
+    order = sorted(range(1, owners), key=lambda k: send_order(k, near))
+    for k in order:
+        place = map_ref[flip(me, k)]
+        thick, pressure = thick_block(place), surface[0, place]
+        for c in range(pieces):
+            outgoing[k, c, 0], outgoing[k, c, 1] = cut(thick, c), cut(pressure, c)
+    place = map_ref[me]
+    thick, pressure = thick_block(place), surface[0, place]
+    for c in range(pieces):
+        arrived[c, me, 0], arrived[c, me, 1] = cut(thick, c), cut(pressure, c)
+    pl.semaphore_wait(barrier, owners)
     block_copies = {}
-    order = sorted(range(1, owners), key=lambda k: SEND_ORDER(k, near))
-    for k in order:
-        peer = flip(me, k)
-        place = map_ref[peer]
-        outgoing[k, 0] = thick_block(place)
-        outgoing[k, 1] = surface[0, place]
-        block_copies[k] = remote(
-            outgoing.at[k], arrived.at[me], block_send.at[k], block_recv.at[k], cfd=peer
-        )
-        block_copies[k].start()
-    place = map_ref[me]
-    arrived[me, 0] = thick_block(place)
-    arrived[me, 1] = surface[0, place]
+    for c in range(pieces):
+        for k in order:
+            block_copies[c, k] = remote(
+                outgoing.at[k, c],
+                arrived.at[c, me],
+                block_send.at[k, c],
+                block_recv.at[k, c],
+                cfd=flip(me, k),
+            )
+            block_copies[c, k].start()
 
     ids = ids_ref[...]
     down = jnp.concatenate([ids, jnp.zeros((LANES - bands, width), jnp.int32)], axis=0).T
@@ -301,28 +315,53 @@
     get_inverse = pltpu.make_async_copy(found, inverse, load_sems.at[2])
     get_inverse.start()
 
-    step = lax.broadcasted_iota(jnp.int32, (near * size, steps), 1)
-
-    def rate(series):
-        moved = jnp.where(step > 0, series - pltpu.roll(series, 1, 1), 0.0)
-        return moved.astype(jnp.bfloat16).astype(jnp.float32)
-
-    for j in [0, 1] + list(range(2, zs)):
-        for k in range(near * j, near * j + near):
-            if k:
-                block_copies[k].wait()
-        first = flip(z, j) * near
-        series = arrived[pl.ds(first, near)].astype(jnp.float32)
-        thick = series[:, 0].reshape(near * size, steps)
-        pressure = series[:, 1].reshape(near * size, steps)
-        for c, value in enumerate((rate(thick), rate(pressure), pressure)):
-            for k in range(taps):
-                late = pltpu.roll(value, k, 1) if k else value
-                top = (k * terms + c) * faces + first * size
-                here = pl.ds(pl.multiple_of(top, near * size), near * size)
-                for t in range(steps // LANES):
-                    sources[t, here, :] = late[:, t * LANES : (t + 1) * LANES].astype(jnp.bfloat16)
-    get_weights.wait()
+    start_lane = lax.broadcasted_iota(jnp.int32, (faces, LANES), 1) == 0
+    rows_each = 4 * width
+
+    def source_tile(c, u):
+        tile = c * (span // LANES) + u
+        lanes = slice(u * LANES, (u + 1) * LANES)
+
+        def late(value, place):
+            turned = pltpu.roll(value, 1, 1)
+            moved = jnp.where(start_lane, before[place], turned) if tile else turned
+            before[place] = turned
+            return moved
+
+        for n in range(2):
+            value = arrived[c, :, n, :, lanes].astype(jnp.float32).reshape(faces, LANES)
+            last = late(value, 2 * n)
+            rate = value - last
+            if tile == 0:
+                rate = jnp.where(start_lane, 0.0, rate)
+            rate = rate.astype(jnp.bfloat16).astype(jnp.float32)
+            taken = [(n, rate, late(rate, 2 * n + 1))]
+            if n == 1:
+                taken.append((2, value, last))
+            for term, now, then in taken:
+                for k, series in enumerate((now, then)):
+                    here = pl.ds((k * terms + term) * faces, faces)
+                    sources[here, lanes] = series.astype(jnp.bfloat16)
+
+    for c in range(pieces):
+        for k in order:
+            block_copies[c, k].wait()
+        for u in range(span // LANES):
+            source_tile(c, u)
+        if c == 0:
+            get_weights.wait()
+
+        @pl.loop(0, observers // rows_each)
+        def _(part):
+            here = pl.ds(pl.multiple_of(part * rows_each, rows_each), rows_each)
+            chosen = jnp.concatenate(
+                [weights[k, t, here, :] for k in range(taps) for t in range(terms)], axis=1
+            )
+            product = jnp.dot(chosen, sources[...], preferred_element_type=jnp.float32)
+            for u in range(span // LANES):
+                wide[c * (span // LANES) + u, pl.ds(part * 4, 4)] = product[
+                    :, u * LANES : (u + 1) * LANES
+                ].reshape(4, width, LANES)
 
     @pl.loop(0, bands)
     def _(b):
@@ -330,15 +369,7 @@
         tile = jnp.minimum(lax.div(start, LANES), steps // LANES - chunks - 1)
         rest = start - tile * LANES
         shift = lax.rem(LANES - rest, LANES)
-        here = pl.ds(pl.multiple_of(b * width, width), width)
-        chosen = jnp.concatenate(
-            [weights[k, c, here, :] for k in range(taps) for c in range(terms)], axis=1
-        )
-        window = jnp.concatenate([sources[tile + t] for t in range(chunks + 1)], axis=1)
-        whole = jnp.dot(chosen, window, preferred_element_type=jnp.float32)
-        parts = [
-            pltpu.roll(whole[:, t * LANES : (t + 1) * LANES], shift, 1) for t in range(chunks + 1)
-        ]
+        parts = [pltpu.roll(wide[tile + t, b], shift, 1) for t in range(chunks + 1)]
         for t in range(chunks):
             slots[pl.ds(b * (width * chunks) + t, width, stride=chunks), :] = jnp.where(
                 lane < LANES - rest, parts[t], parts[t + 1]
@@ -348,15 +379,14 @@
     unroll = 32
 
     def gather(owner):
-        base = owner * height
-
         @pl.loop(0, height // unroll)
         def _(group):
-            for m in range(unroll):
-                at = base + group * unroll + m
-                found_at = inverse[lax.div(at, LANES), lax.rem(at, LANES)]
-                value = slots.reshape(observers, chunks, LANES)[found_at]
-                rows[pl.ds(pl.multiple_of(at * chunks, chunks), chunks), :] = value
+            first = group * unroll
+            places = [inverse[owner, first + m] for m in range(unroll)]
+            values = [slots.reshape(observers, chunks, LANES)[place] for place in places]
+            top = pl.multiple_of((owner * height + first) * chunks, unroll * chunks)
+            for m, value in enumerate(values):
+                rows[pl.ds(top + m * chunks, chunks), :] = value
 
     def unit(owner, t):
         return rows[pl.ds(owner * (height * chunks) + t, height, stride=chunks), :]
@@ -439,24 +469,26 @@
         )
         z_copies[j].start()
 
-    for place, j in enumerate(turn):
-        send_core(j)
-        if place:
-            send_first(turn[place - 1])
-    send_first(turn[-1])
-    for j in turn:
-        send_second(j)
-    for j in turn[:-1]:
-        send_z(j)
+    for step in range(zs + 4):
+        if step < zs:
+            send_core(turn[step])
+        if 1 <= step < zs:
+            send_first(turn[step - 1])
+        if 3 <= step < zs + 3:
+            send_second(turn[step - 3])
+        if step == zs:
+            send_first(turn[-1])
+        if 4 <= step < zs + 3:
+            send_z(turn[step - 4])
     results = list(finish_second(0))
     for j in turn[:-1]:
         z_copies[j].wait()
         results = [value + wide_of(z_in[j, s]) for s, value in enumerate(results)]
-    for s, value in enumerate(results):
-        out_ref[:, s * LANES : (s + 1) * LANES] = value
-
-
-def SEND_ORDER(k, near):
+    for value, result_ref in zip(results, (first_ref, second_ref)):
+        result_ref[...] = value
+
+
+def send_order(k, near):
     j = k // near
     return (0, 3, 1, 2)[j] if j < 4 else j, k
 
@@ -476,18 +508,22 @@
     vmem, smem, hbm = (
         pl.BlockSpec(memory_space=space) for space in (pltpu.VMEM, pltpu.SMEM, pl.ANY)
     )
-    return pl.pallas_call(
+    pieces = 4
+    span = steps // pieces
+    first, second = pl.pallas_call(
         fused_kernel,
-        out_shape=jax.ShapeDtypeStruct((height, chunks // halves * LANES), f32),
+        out_shape=[jax.ShapeDtypeStruct(tile, f32)] * 2,
         in_specs=[smem, smem, vmem, vmem, hbm, hbm],
-        out_specs=vmem,
+        out_specs=[vmem, vmem],
         scratch_shapes=[
             pltpu.VMEM((surface_raw.shape[0], owners, size, steps), bf16),
             pltpu.VMEM(kernel_weights.shape, bf16),
             pltpu.VMEM((owners, size, LANES), f32),
-            pltpu.VMEM((owners, 2, size, steps), bf16),
-            pltpu.VMEM((owners, 2, size, steps), bf16),
-            pltpu.VMEM((steps // LANES, taps * terms * faces, LANES), bf16),
+            pltpu.VMEM((owners, pieces, 2, size, span), bf16),
+            pltpu.VMEM((pieces, owners, 2, size, span), bf16),
+            pltpu.VMEM((taps * terms * faces, span), bf16),
+            pltpu.VMEM((4,) + tile, f32),
+            pltpu.VMEM((steps // LANES, bands, width, LANES), f32),
             pltpu.VMEM((bands, width, LANES), i32),
             pltpu.VMEM((observers // LANES, LANES), i32),
             pltpu.SMEM((observers // LANES, LANES), i32),
@@ -506,8 +542,8 @@
             pltpu.VMEM((zs, 2) + tile, bf16),
             pltpu.VMEM((zs, 2) + tile, bf16),
             dma((3,)),
-            dma((owners,)),
-            dma((owners,)),
+            dma((owners, pieces)),
+            dma((owners, pieces)),
             dma((zs,)),
             dma((zs,)),
             dma((2, zs)),
@@ -529,6 +565,7 @@
         surface_raw.reshape(surface_raw.shape[0], owners, size, steps),
         kernel_weights,
     )
+    return jnp.concatenate([first, second], axis=1)
 
 
 def fits_fused(owners, halves, surface_raw, kernel_weights, band_observers):
@@ -542,7 +579,8 @@
         and band_observers.shape[1] == LANES
         and faces // owners % 8 == 0
         and steps == 2 * tiles * LANES
-        and kernel_weights.shape[2] % (owners * 32) == 0
+        and kernel_weights.shape[:1] + kernel_weights.shape[2:3] == (2, owners * LANES)
+        and band_observers.shape[0] % 4 == 0
     )
 
 

time: 52.2 us -> 45.9 us (0.88)
  Pallas kernels: 50.4 us -> 44.2 us
  local copies, waits for them, and re-layouts: 1.57 us -> 0 us
  other arithmetic: 0 us -> 1.54 us
    pallas_call x1, Pallas kernels: 50.4 us -> 44.2 us  [fused(): pl.pallas_call(fused_kernel, out_shape=[jax.ShapeDtypeStruct(tile, f32)]...]
    unnamed x1 -> x0, local copies, waits for them, and re-layouts: 1.57 us -> none
    concatenate x0 -> x1, other arithmetic: none -> 1.54 us  [fused(): return jnp.concatenate([first, second], axis=1)]
where the time goes in v2:
time: 45.9 us; the launch traced here: 45.7 us
  Pallas kernels  44.2 us (96%)
  other arithmetic  1.54 us (3%)
    pallas_call x1, Pallas kernels, fused(): pl.pallas_call(fused_kernel, out_shape=[jax.ShapeDtypeStruct(tile, f32)]...  44.2 us
    concatenate x1, other arithmetic, fused(): return jnp.concatenate([first, second], axis=1)  1.54 us

profile of v2, /device:TPU:0, one launch (start us, length us, event | category | flops | bytes accessed | tf_op | source)
XLA Modules:
  0.0 45.7 jit_solution(12845921032900004505)
XLA Ops:
  0.0 44.2 %fused.1 = (f32[128,128]{1,0:T(8,128)}, f32[128,128]{1,0:T(8,128)}) custom-call(s32[16]{0:T(128)} %lags_ref.1, s32[16]{0:T(128)} %bitcast.3, s32[16,128]{1,0:T(8,128)} %ids_ref.1, bf16[3,128]{1,0:T(4,128)(2,1)} %normals_ref.1, bf16[5,16,8,1024]{3,2,1,0:T(8,128)(2,1)} %bitcast.2, bf16[2,3,2048,128]{3,2,1,0:T(8,128)(2,1)} %weights_ref.1), custom_call_target="tpu_custom_call" | custom-call | tf_op jit(solution)/shard_map/fused/pallas_call | solution.py:513
  44.2 1.5 %pad_maximum_fusion = f32[128,256]{1,0:T(8,128)} fusion(f32[128,128]{1,0:T(8,128)} %get-tuple-element.8, f32[128,128]{1,0:T(8,128)} %get-tuple-element.7), kind=kLoop, calls=%fused_computation | loop fusion | flops 32768 | bytes 262144 | tf_op jit(solution)/shard_map/concatenate | solution.py:568

commit v3 on v2

--- a/solution.py
+++ b/solution.py
@@ -190,6 +190,10 @@
     weights_ref,
     first_ref,
     second_ref,
+    lags,
+    block_at,
+    ids_here,
+    flat_normals,
     surface,
     weights,
     normals,
@@ -234,7 +238,7 @@
     core, x, z = lax.rem(me, 2), lax.rem(lax.div(me, 2), 2), lax.div(me, 4)
     y = lax.axis_index("ac")
     taps, terms, observers, faces = weights.shape
-    bands, width = ids_ref.shape
+    bands, width = ids_here.shape
     size, steps = surface.shape[2:]
     out_len = steps // 2
     chunks = out_len // LANES
@@ -244,6 +248,19 @@
     get_surface = pltpu.make_async_copy(surface_ref, surface, load_sems.at[0])
     get_weights = pltpu.make_async_copy(weights_ref, weights, load_sems.at[1])
     get_surface.start()
+    small = [
+        pltpu.make_async_copy(src, dst, load_sems.at[3 + n])
+        for n, (src, dst) in enumerate(
+            (
+                (normals_ref, flat_normals),
+                (map_ref, block_at),
+                (ids_ref, ids_here),
+                (lags_ref, lags),
+            )
+        )
+    ]
+    for copy in small:
+        copy.start()
 
     def remote(src, dst, send, recv, **peer):
         return pltpu.make_async_remote_copy(
@@ -258,7 +275,9 @@
         )
     pl.semaphore_signal(barrier, inc=1, device_id={"ac": 1 - y}, device_id_type=pl.DeviceIdType.MESH)
 
-    flat = normals_ref[...].astype(jnp.float32)
+    for copy in small:
+        copy.wait()
+    flat = flat_normals[...].astype(jnp.float32)
     tall = jnp.concatenate([flat, jnp.zeros((LANES - flat.shape[0], faces), jnp.float32)], axis=0)
     normals[...] = tall.T.reshape(owners, size, LANES)
     get_surface.wait()
@@ -275,11 +294,11 @@
 
     order = sorted(range(1, owners), key=lambda k: send_order(k, near))
     for k in order:
-        place = map_ref[flip(me, k)]
+        place = block_at[flip(me, k)]
         thick, pressure = thick_block(place), surface[0, place]
         for c in range(pieces):
             outgoing[k, c, 0], outgoing[k, c, 1] = cut(thick, c), cut(pressure, c)
-    place = map_ref[me]
+    place = block_at[me]
     thick, pressure = thick_block(place), surface[0, place]
     for c in range(pieces):
         arrived[c, me, 0], arrived[c, me, 1] = cut(thick, c), cut(pressure, c)
@@ -296,7 +315,7 @@
             )
             block_copies[c, k].start()
 
-    ids = ids_ref[...]
+    ids = ids_here[...]
     down = jnp.concatenate([ids, jnp.zeros((LANES - bands, width), jnp.int32)], axis=0).T
     for b in range(bands):
         spread[b] = jnp.broadcast_to(down[:, b : b + 1], (width, LANES))
@@ -316,7 +335,8 @@
     get_inverse.start()
 
     start_lane = lax.broadcasted_iota(jnp.int32, (faces, LANES), 1) == 0
-    rows_each = 4 * width
+    bands_each = 8
+    rows_each = bands_each * width
 
     def source_tile(c, u):
         tile = c * (span // LANES) + u
@@ -359,13 +379,12 @@
             )
             product = jnp.dot(chosen, sources[...], preferred_element_type=jnp.float32)
             for u in range(span // LANES):
-                wide[c * (span // LANES) + u, pl.ds(part * 4, 4)] = product[
+                wide[c * (span // LANES) + u, pl.ds(part * bands_each, bands_each)] = product[
                     :, u * LANES : (u + 1) * LANES
-                ].reshape(4, width, LANES)
-
-    @pl.loop(0, bands)
-    def _(b):
-        start = out_len - lags_ref[b]
+                ].reshape(bands_each, width, LANES)
+
+    def shift_band(b):
+        start = out_len - lags[b]
         tile = jnp.minimum(lax.div(start, LANES), steps // LANES - chunks - 1)
         rest = start - tile * LANES
         shift = lax.rem(LANES - rest, LANES)
@@ -375,18 +394,24 @@
                 lane < LANES - rest, parts[t], parts[t + 1]
             )
 
+    @pl.loop(0, bands // 4)
+    def _(group):
+        for m in range(4):
+            shift_band(group * 4 + m)
+
     get_inverse.wait()
     unroll = 32
 
-    def gather(owner):
-        @pl.loop(0, height // unroll)
-        def _(group):
-            first = group * unroll
-            places = [inverse[owner, first + m] for m in range(unroll)]
-            values = [slots.reshape(observers, chunks, LANES)[place] for place in places]
-            top = pl.multiple_of((owner * height + first) * chunks, unroll * chunks)
-            for m, value in enumerate(values):
-                rows[pl.ds(top + m * chunks, chunks), :] = value
+    def gather(top, side):
+        @pl.loop(0, 2)
+        def _(other):
+            owner = top + other * 2 + side
+            base = pl.multiple_of(owner * (height * chunks), height * chunks)
+            for first in range(0, height, unroll):
+                places = [inverse[owner, first + m] for m in range(unroll)]
+                values = [slots.reshape(observers, chunks, LANES)[place] for place in places]
+                for m, value in enumerate(values):
+                    rows[pl.ds(base + (first + m) * chunks, chunks), :] = value
 
     def unit(owner, t):
         return rows[pl.ds(owner * (height * chunks) + t, height, stride=chunks), :]
@@ -403,8 +428,7 @@
 
     def send_core(j):
         top = flip(z, j) * near
-        for other in range(2):
-            gather(top + other * 2 + 1 - core)
+        gather(top, 1 - core)
         for other in range(2):
             for t in range(chunks):
                 core_out[j, other, t] = narrow(unit(top + other * 2 + 1 - core, t))
@@ -412,8 +436,7 @@
             core_out.at[j], core_in.at[j], core_send.at[j], core_recv.at[j], cfd=flip(me, 1)
         )
         core_copies[j].start()
-        for other in range(2):
-            gather(top + other * 2 + core)
+        gather(top, core)
 
     def send_first(j):
         top = flip(z, j) * near
@@ -505,17 +528,19 @@
     bf16, f32, i32 = jnp.bfloat16, jnp.float32, jnp.int32
     tile = (height, LANES)
     dma = pltpu.SemaphoreType.DMA
-    vmem, smem, hbm = (
-        pl.BlockSpec(memory_space=space) for space in (pltpu.VMEM, pltpu.SMEM, pl.ANY)
-    )
+    vmem, hbm = (pl.BlockSpec(memory_space=space) for space in (pltpu.VMEM, pltpu.HBM))
     pieces = 4
     span = steps // pieces
     first, second = pl.pallas_call(
         fused_kernel,
         out_shape=[jax.ShapeDtypeStruct(tile, f32)] * 2,
-        in_specs=[smem, smem, vmem, vmem, hbm, hbm],
+        in_specs=[hbm] * 6,
         out_specs=[vmem, vmem],
         scratch_shapes=[
+            pltpu.SMEM((bands,), i32),
+            pltpu.SMEM((owners,), i32),
+            pltpu.VMEM((bands, width), i32),
+            pltpu.VMEM(area_normals.shape, bf16),
             pltpu.VMEM((surface_raw.shape[0], owners, size, steps), bf16),
             pltpu.VMEM(kernel_weights.shape, bf16),
             pltpu.VMEM((owners, size, LANES), f32),
@@ -541,7 +566,7 @@
             pltpu.VMEM((2, zs) + tile, bf16),
             pltpu.VMEM((zs, 2) + tile, bf16),
             pltpu.VMEM((zs, 2) + tile, bf16),
-            dma((3,)),
+            dma((7,)),
             dma((owners, pieces)),
             dma((owners, pieces)),
             dma((zs,)),
@@ -554,16 +579,21 @@
             dma((zs,)),
         ],
         compiler_params=pltpu.CompilerParams(
-            collective_id=0, has_side_effects=True, vmem_limit_bytes=60 * 2**20
+            collective_id=0, has_side_effects=True, vmem_limit_bytes=40 * 2**20
         ),
         name="fused",
     )(
-        band_lags,
-        block_map[0, 0],
-        band_observers,
-        area_normals,
-        surface_raw.reshape(surface_raw.shape[0], owners, size, steps),
-        kernel_weights,
+        *(
+            pltpu.with_memory_space_constraint(value, pltpu.HBM)
+            for value in (
+                band_lags,
+                block_map[0, 0],
+                band_observers,
+                area_normals,
+                surface_raw.reshape(surface_raw.shape[0], owners, size, steps),
+                kernel_weights,
+            )
+        )
     )
     return jnp.concatenate([first, second], axis=1)
 
@@ -580,7 +610,7 @@
         and faces // owners % 8 == 0
         and steps == 2 * tiles * LANES
         and kernel_weights.shape[:1] + kernel_weights.shape[2:3] == (2, owners * LANES)
-        and band_observers.shape[0] % 4 == 0
+        and band_observers.shape[0] % 8 == 0
     )
 
 

time: 45.9 us -> 41 us (0.89)
  Pallas kernels: 44.2 us -> 40.2 us
  other arithmetic: 1.54 us -> 0.67 us
    pallas_call x1, Pallas kernels: 44.2 us -> 40.2 us  [fused(): pl.pallas_call(fused_kernel, out_shape=[jax.ShapeDtypeStruct(tile, f32)]...]
    concatenate x1, other arithmetic: 1.54 us -> 0.67 us  [fused(): return jnp.concatenate([first, second], axis=1)]
where the time goes in v3:
time: 41 us; the launch traced here: 40.9 us
  Pallas kernels  40.2 us (98%)
  other arithmetic  0.67 us (2%)
    pallas_call x1, Pallas kernels, fused(): pl.pallas_call(fused_kernel, out_shape=[jax.ShapeDtypeStruct(tile, f32)]...  40.2 us

profile of v3, /device:TPU:0, one launch (start us, length us, event | category | flops | bytes accessed | tf_op | source)
XLA Modules:
  0.0 40.9 jit_solution(13912882864761472245)
XLA Ops:
  0.0 40.2 %fused.1 = (f32[128,128]{1,0:T(8,128)S(1)}, f32[128,128]{1,0:T(8,128)S(1)}) custom-call(s32[16]{0:T(128)} %lags_ref.1, s32[16]{0:T(128)} %bitcast.3, s32[16,128]{1,0:T(8,128)} %ids_ref.1, bf16[3,128]{1,0:T(4,128)(2,1)} %normals_ref.1, bf16[5,16,8,1024]{3,2,1,0:T(8,128)(2,1)} %bitcast.2, bf16[2,3,2048,128]{3,2,1,0:T(8,128)(2,1)} %weights_ref.1), custom_call_target="tpu_custom_call" | custom-call | tf_op jit(solution)/shard_map/fused/pallas_call | solution.py:534
  40.2 0.7 %pad_maximum_fusion = f32[128,256]{1,0:T(8,128)} fusion(f32[128,128]{1,0:T(8,128)S(1)} %get-tuple-element.8, f32[128,128]{1,0:T(8,128)S(1)} %get-tuple-element.7), kind=kLoop, calls=%fused_computation | loop fusion | flops 32768 | bytes 262144 | tf_op jit(solution)/shard_map/concatenate | solution.py:598

commit v4 on v3

--- a/solution.py
+++ b/solution.py
@@ -243,6 +243,7 @@
     out_len = steps // 2
     chunks = out_len // LANES
     height = observers // owners
+    half = chunks // 2
     near = owners // zs
 
     get_surface = pltpu.make_async_copy(surface_ref, surface, load_sems.at[0])
@@ -283,6 +284,9 @@
     get_surface.wait()
     get_weights.start()
 
+    def wait_all(ref, sem):
+        pltpu.make_async_copy(ref, ref, sem).wait()
+
     def thick_block(place):
         along = surface[2, place].astype(jnp.float32) * normals[place, :, 0:1]
         along = along + surface[3, place].astype(jnp.float32) * normals[place, :, 1:2]
@@ -303,17 +307,15 @@
     for c in range(pieces):
         arrived[c, me, 0], arrived[c, me, 1] = cut(thick, c), cut(pressure, c)
     pl.semaphore_wait(barrier, owners)
-    block_copies = {}
     for c in range(pieces):
         for k in order:
-            block_copies[c, k] = remote(
+            remote(
                 outgoing.at[k, c],
                 arrived.at[c, me],
-                block_send.at[k, c],
-                block_recv.at[k, c],
+                block_send.at[0],
+                block_recv.at[c],
                 cfd=flip(me, k),
-            )
-            block_copies[c, k].start()
+            ).start()
 
     ids = ids_here[...]
     down = jnp.concatenate([ids, jnp.zeros((LANES - bands, width), jnp.int32)], axis=0).T
@@ -363,9 +365,21 @@
                     here = pl.ds((k * terms + term) * faces, faces)
                     sources[here, lanes] = series.astype(jnp.bfloat16)
 
+    def shift_band(b, first, last):
+        start = out_len - lags[b]
+        tile = jnp.minimum(lax.div(start, LANES), steps // LANES - chunks - 1)
+        rest = start - tile * LANES
+        shift = lax.rem(LANES - rest, LANES)
+        parts = [pltpu.roll(wide[tile + t, b], shift, 1) for t in range(first, last + 1)]
+        early = lane[:8] < LANES - rest
+        for top in range(0, width, 8):
+            for t in range(first, last):
+                now, then = (parts[t - first + n][top : top + 8] for n in range(2))
+                here = pl.ds(b * (width * chunks) + top * chunks + t, 8, stride=chunks)
+                slots[here, :] = jnp.where(early, now, then)
+
     for c in range(pieces):
-        for k in order:
-            block_copies[c, k].wait()
+        wait_all(arrived.at[c, pl.ds(0, owners - 1)], block_recv.at[c])
         for u in range(span // LANES):
             source_tile(c, u)
         if c == 0:
@@ -373,6 +387,9 @@
 
         @pl.loop(0, observers // rows_each)
         def _(part):
+            if c == pieces - 1:
+                for m in range(bands_each):
+                    shift_band(part * bands_each + m, 0, half)
             here = pl.ds(pl.multiple_of(part * rows_each, rows_each), rows_each)
             chosen = jnp.concatenate(
                 [weights[k, t, here, :] for k in range(taps) for t in range(terms)], axis=1
@@ -383,21 +400,10 @@
                     :, u * LANES : (u + 1) * LANES
                 ].reshape(bands_each, width, LANES)
 
-    def shift_band(b):
-        start = out_len - lags[b]
-        tile = jnp.minimum(lax.div(start, LANES), steps // LANES - chunks - 1)
-        rest = start - tile * LANES
-        shift = lax.rem(LANES - rest, LANES)
-        parts = [pltpu.roll(wide[tile + t, b], shift, 1) for t in range(chunks + 1)]
-        for t in range(chunks):
-            slots[pl.ds(b * (width * chunks) + t, width, stride=chunks), :] = jnp.where(
-                lane < LANES - rest, parts[t], parts[t + 1]
-            )
-
     @pl.loop(0, bands // 4)
     def _(group):
         for m in range(4):
-            shift_band(group * 4 + m)
+            shift_band(group * 4 + m, half, chunks)
 
     get_inverse.wait()
     unroll = 32
@@ -422,8 +428,7 @@
     def wide_of(value):
         return value.astype(jnp.float32)
 
-    half = chunks // 2
-    core_copies, x_copies, y_copies, xy_copies, yx_copies, z_copies = {}, {}, {}, {}, {}, {}
+    core_copies, x_copies, y_copies, xy_copies, yx_copies = {}, {}, {}, {}, {}
     turn = list(range(2, zs)) + [1, 0]
 
     def send_core(j):
@@ -433,79 +438,96 @@
             for t in range(chunks):
                 core_out[j, other, t] = narrow(unit(top + other * 2 + 1 - core, t))
         core_copies[j] = remote(
-            core_out.at[j], core_in.at[j], core_send.at[j], core_recv.at[j], cfd=flip(me, 1)
+            core_out.at[j], core_in.at[j], core_send.at[0], core_recv.at[j], cfd=flip(me, 1)
         )
         core_copies[j].start()
         gather(top, core)
 
     def send_first(j):
         top = flip(z, j) * near
-        core_copies[j].wait()
+        core_copies[j].wait_recv()
 
         def total(other, t):
             return unit(top + other * 2 + core, t) + wide_of(core_in[j, other, t])
 
-        for side in range(2):
+        for n, (side, other) in enumerate(((1 - y, 1 - x), (y, x))):
             x_out[j, side] = narrow(total(1 - x, side * half))
-        x_copies[j] = remote(
-            x_out.at[j], x_in.at[j], first_send.at[0, j], first_recv.at[0, j], cfd=flip(me, 2)
-        )
-        x_copies[j].start()
-        for other in range(2):
+            x_copies[j, n] = remote(
+                x_out.at[j, side],
+                x_in.at[j, side],
+                first_send.at[0],
+                first_recv.at[0, n, j],
+                cfd=flip(me, 2),
+            )
+            x_copies[j, n].start()
             y_out[j, other] = narrow(total(other, (1 - y) * half + 1))
-        y_copies[j] = remote(
-            y_out.at[j], y_in.at[j], first_send.at[1, j], first_recv.at[1, j], ac=1 - y
-        )
-        y_copies[j].start()
+            y_copies[j, n] = remote(
+                y_out.at[j, other],
+                y_in.at[j, other],
+                first_send.at[1],
+                first_recv.at[1, n, j],
+                ac=1 - y,
+            )
+            y_copies[j, n].start()
         for side in range(2):
             x_kept[j, side] = total(x, side * half)
         for other in range(2):
             y_kept[j, other] = total(other, y * half + 1)
 
     def send_second(j):
-        x_copies[j].wait()
+        x_copies[j, 0].wait_recv()
         xy_out[0, j] = narrow(x_kept[j, 1 - y] + wide_of(x_in[j, 1 - y]))
         xy_copies[j] = remote(
-            xy_out.at[0, j], xy_in.at[0, j], second_send.at[0, j], second_recv.at[0, j], ac=1 - y
+            xy_out.at[0, j], xy_in.at[0, j], second_send.at[0], second_recv.at[0, j], ac=1 - y
         )
         xy_copies[j].start()
-        y_copies[j].wait()
+        y_copies[j, 0].wait_recv()
         xy_out[1, j] = narrow(y_kept[j, 1 - x] + wide_of(y_in[j, 1 - x]))
         yx_copies[j] = remote(
-            xy_out.at[1, j], xy_in.at[1, j], second_send.at[1, j], second_recv.at[1, j],
+            xy_out.at[1, j],
+            xy_in.at[1, j],
+            second_send.at[0],
+            second_recv.at[1, j],
             cfd=flip(me, 2),
         )
         yx_copies[j].start()
 
     def finish_second(j):
-        xy_copies[j].wait()
+        x_copies[j, 1].wait_recv()
+        xy_copies[j].wait_recv()
         from_x = x_kept[j, y] + wide_of(x_in[j, y]) + wide_of(xy_in[0, j])
-        yx_copies[j].wait()
+        y_copies[j, 1].wait_recv()
+        yx_copies[j].wait_recv()
         from_y = y_kept[j, x] + wide_of(y_in[j, x]) + wide_of(xy_in[1, j])
         return from_x, from_y
 
     def send_z(j):
         for stream, value in enumerate(finish_second(j)):
             z_out[j, stream] = narrow(value)
-        z_copies[j] = remote(
-            z_out.at[j], z_in.at[j], z_send.at[j], z_recv.at[j], cfd=flip(me, near * j)
-        )
-        z_copies[j].start()
-
-    for step in range(zs + 4):
+        remote(
+            z_out.at[j], z_in.at[j], z_send.at[0], z_recv.at[0], cfd=flip(me, near * j)
+        ).start()
+
+    for step in range(zs + 5):
         if step < zs:
             send_core(turn[step])
-        if 1 <= step < zs:
+        if 1 <= step < zs - 1:
             send_first(turn[step - 1])
         if 3 <= step < zs + 3:
             send_second(turn[step - 3])
-        if step == zs:
-            send_first(turn[-1])
+        if zs - 1 <= step < zs + 1:
+            send_first(turn[step - 1])
         if 4 <= step < zs + 3:
             send_z(turn[step - 4])
     results = list(finish_second(0))
+    wait_all(outgoing.at[pl.ds(1, owners - 1)], block_send.at[0])
+    wait_all(core_out, core_send.at[0])
+    wait_all(x_out, first_send.at[0])
+    wait_all(y_out, first_send.at[1])
+    wait_all(xy_out, second_send.at[0])
+    wait_all(z_out.at[pl.ds(1, zs - 1)], z_send.at[0])
+    wait_all(z_in.at[pl.ds(1, zs - 1)], z_recv.at[0])
     for j in turn[:-1]:
-        z_copies[j].wait()
         results = [value + wide_of(z_in[j, s]) for s, value in enumerate(results)]
     for value, result_ref in zip(results, (first_ref, second_ref)):
         result_ref[...] = value
@@ -567,16 +589,16 @@
             pltpu.VMEM((zs, 2) + tile, bf16),
             pltpu.VMEM((zs, 2) + tile, bf16),
             dma((7,)),
-            dma((owners, pieces)),
-            dma((owners, pieces)),
+            dma((1,)),
+            dma((pieces,)),
+            dma((1,)),
             dma((zs,)),
-            dma((zs,)),
+            dma((2,)),
+            dma((2, 2, zs)),
+            dma((1,)),
             dma((2, zs)),
-            dma((2, zs)),
-            dma((2, zs)),
-            dma((2, zs)),
-            dma((zs,)),
-            dma((zs,)),
+            dma((1,)),
+            dma((1,)),
         ],
         compiler_params=pltpu.CompilerParams(
             collective_id=0, has_side_effects=True, vmem_limit_bytes=40 * 2**20

time: 41 us -> 38.8 us (0.946)
  Pallas kernels: 40.2 us -> 38 us
    pallas_call x1, Pallas kernels: 40.2 us -> 38 us  [fused(): pl.pallas_call(fused_kernel, out_shape=[jax.ShapeDtypeStruct(tile, f32)]...]
where the time goes in v4:
time: 38.8 us; the launch traced here: 38.7 us
  Pallas kernels  38 us (98%)
  other arithmetic  0.67 us (2%)
    pallas_call x1, Pallas kernels, fused(): pl.pallas_call(fused_kernel, out_shape=[jax.ShapeDtypeStruct(tile, f32)]...  38 us

profile of v4, /device:TPU:0, one launch (start us, length us, event | category | flops | bytes accessed | tf_op | source)
XLA Modules:
  0.0 38.7 jit_solution(856903252837588979)
XLA Ops:
  0.0 38.0 %fused.1 = (f32[128,128]{1,0:T(8,128)S(1)}, f32[128,128]{1,0:T(8,128)S(1)}) custom-call(s32[16]{0:T(128)} %lags_ref.1, s32[16]{0:T(128)} %bitcast.3, s32[16,128]{1,0:T(8,128)} %ids_ref.1, bf16[3,128]{1,0:T(4,128)(2,1)} %normals_ref.1, bf16[5,16,8,1024]{3,2,1,0:T(8,128)(2,1)} %bitcast.2, bf16[2,3,2048,128]{3,2,1,0:T(8,128)(2,1)} %weights_ref.1), custom_call_target="tpu_custom_call" | custom-call | tf_op jit(solution)/shard_map/fused/pallas_call | solution.py:556
  38.0 0.7 %pad_maximum_fusion = f32[128,256]{1,0:T(8,128)} fusion(f32[128,128]{1,0:T(8,128)S(1)} %get-tuple-element.8, f32[128,128]{1,0:T(8,128)S(1)} %get-tuple-element.7), kind=kLoop, calls=%fused_computation | loop fusion | flops 32768 | bytes 262144 | tf_op jit(solution)/shard_map/concatenate | solution.py:620

commit v5 on v4

--- a/solution.py
+++ b/solution.py
@@ -370,13 +370,13 @@
         tile = jnp.minimum(lax.div(start, LANES), steps // LANES - chunks - 1)
         rest = start - tile * LANES
         shift = lax.rem(LANES - rest, LANES)
-        parts = [pltpu.roll(wide[tile + t, b], shift, 1) for t in range(first, last + 1)]
-        early = lane[:8] < LANES - rest
+        early = lane[:8] >= rest
         for top in range(0, width, 8):
+            tiles = [wide[tile + t, b, top : top + 8] for t in range(first, last + 1)]
             for t in range(first, last):
-                now, then = (parts[t - first + n][top : top + 8] for n in range(2))
                 here = pl.ds(b * (width * chunks) + top * chunks + t, 8, stride=chunks)
-                slots[here, :] = jnp.where(early, now, then)
+                mixed = jnp.where(early, tiles[t - first], tiles[t - first + 1])
+                slots[here, :] = pltpu.roll(mixed, shift, 1)
 
     for c in range(pieces):
         wait_all(arrived.at[c, pl.ds(0, owners - 1)], block_recv.at[c])
@@ -429,7 +429,6 @@
         return value.astype(jnp.float32)
 
     core_copies, x_copies, y_copies, xy_copies, yx_copies = {}, {}, {}, {}, {}
-    turn = list(range(2, zs)) + [1, 0]
 
     def send_core(j):
         top = flip(z, j) * near
@@ -501,24 +500,38 @@
         from_y = y_kept[j, x] + wide_of(y_in[j, x]) + wide_of(xy_in[1, j])
         return from_x, from_y
 
-    def send_z(j):
+    def send_z(j, peer, passed, sems):
         for stream, value in enumerate(finish_second(j)):
+            if passed:
+                z_wait(passed, stream)
+                value = value + wide_of(z_in[passed, stream])
             z_out[j, stream] = narrow(value)
-        remote(
-            z_out.at[j], z_in.at[j], z_send.at[0], z_recv.at[0], cfd=flip(me, near * j)
-        ).start()
-
-    for step in range(zs + 5):
-        if step < zs:
-            send_core(turn[step])
-        if 1 <= step < zs - 1:
-            send_first(turn[step - 1])
-        if 3 <= step < zs + 3:
-            send_second(turn[step - 3])
-        if zs - 1 <= step < zs + 1:
-            send_first(turn[step - 1])
-        if 4 <= step < zs + 3:
-            send_z(turn[step - 4])
+            remote(
+                z_out.at[j, stream],
+                z_in.at[j, stream],
+                z_send.at[0],
+                z_recv.at[sems[stream]],
+                cfd=flip(me, near * peer),
+            ).start()
+
+    def z_wait(j, stream):
+        wait_all(z_in.at[j, stream], z_recv.at[1 + stream])
+
+    send_core(3)
+    send_core(2)
+    send_first(3)
+    send_core(1)
+    send_first(2)
+    send_core(0)
+    send_second(3)
+    send_first(1)
+    send_second(2)
+    send_first(0)
+    send_z(3, 1, 0, (1, 2))
+    send_second(1)
+    send_z(2, 2, 3, (0, 0))
+    send_second(0)
+    send_z(1, 1, 0, (0, 0))
     results = list(finish_second(0))
     wait_all(outgoing.at[pl.ds(1, owners - 1)], block_send.at[0])
     wait_all(core_out, core_send.at[0])
@@ -526,8 +539,8 @@
     wait_all(y_out, first_send.at[1])
     wait_all(xy_out, second_send.at[0])
     wait_all(z_out.at[pl.ds(1, zs - 1)], z_send.at[0])
-    wait_all(z_in.at[pl.ds(1, zs - 1)], z_recv.at[0])
-    for j in turn[:-1]:
+    wait_all(z_in.at[pl.ds(1, 2)], z_recv.at[0])
+    for j in (1, 2):
         results = [value + wide_of(z_in[j, s]) for s, value in enumerate(results)]
     for value, result_ref in zip(results, (first_ref, second_ref)):
         result_ref[...] = value
@@ -598,7 +611,7 @@
             dma((1,)),
             dma((2, zs)),
             dma((1,)),
-            dma((1,)),
+            dma((3,)),
         ],
         compiler_params=pltpu.CompilerParams(
             collective_id=0, has_side_effects=True, vmem_limit_bytes=40 * 2**20
@@ -625,8 +638,7 @@
     tiles = halves * 2
     return (
         halves == 2
-        and owners % 4 == 0
-        and owners & (owners - 1) == 0
+        and owners == 4 * 4
         and faces == LANES
         and band_observers.shape[1] == LANES
         and faces // owners % 8 == 0

time: 38.8 us -> 38.5 us (level)
  no operation moved by 1% of the time
where the time goes in v5:
time: 38.5 us; the launch traced here: 38.4 us
  Pallas kernels  37.7 us (98%)
  other arithmetic  0.67 us (2%)
    pallas_call x1, Pallas kernels, fused(): pl.pallas_call(fused_kernel, out_shape=[jax.ShapeDtypeStruct(tile, f32)]...  37.7 us

profile of v5, /device:TPU:0, one launch (start us, length us, event | category | flops | bytes accessed | tf_op | source)
XLA Modules:
  0.0 38.4 jit_solution(15647197683705821801)
XLA Ops:
  0.0 37.7 %fused.1 = (f32[128,128]{1,0:T(8,128)S(1)}, f32[128,128]{1,0:T(8,128)S(1)}) custom-call(s32[16]{0:T(128)} %lags_ref.1, s32[16]{0:T(128)} %bitcast.3, s32[16,128]{1,0:T(8,128)} %ids_ref.1, bf16[3,128]{1,0:T(4,128)(2,1)} %normals_ref.1, bf16[5,16,8,1024]{3,2,1,0:T(8,128)(2,1)} %bitcast.2, bf16[2,3,2048,128]{3,2,1,0:T(8,128)(2,1)} %weights_ref.1), custom_call_target="tpu_custom_call" | custom-call | tf_op jit(solution)/shard_map/fused/pallas_call | solution.py:569
  37.7 0.7 %pad_maximum_fusion = f32[128,256]{1,0:T(8,128)} fusion(f32[128,128]{1,0:T(8,128)S(1)} %get-tuple-element.8, f32[128,128]{1,0:T(8,128)S(1)} %get-tuple-element.7), kind=kLoop, calls=%fused_computation | loop fusion | flops 32768 | bytes 262144 | tf_op jit(solution)/shard_map/concatenate | solution.py:633

commit v6 on v5

--- a/solution.py
+++ b/solution.py
@@ -239,16 +239,27 @@
     y = lax.axis_index("ac")
     taps, terms, observers, faces = weights.shape
     bands, width = ids_here.shape
-    size, steps = surface.shape[2:]
+    size, steps = surface_ref.shape[2:]
     out_len = steps // 2
     chunks = out_len // LANES
     height = observers // owners
     half = chunks // 2
     near = owners // zs
 
-    get_surface = pltpu.make_async_copy(surface_ref, surface, load_sems.at[0])
+    barrier = pltpu.get_barrier_semaphore()
+    for k in range(owners - 1, 0, -1):
+        pl.semaphore_signal(
+            barrier, inc=1, device_id={"cfd": flip(me, k)}, device_id_type=pl.DeviceIdType.MESH
+        )
+    pl.semaphore_signal(barrier, inc=1, device_id={"ac": 1 - y}, device_id_type=pl.DeviceIdType.MESH)
+
+    get_surface = [
+        pltpu.make_async_copy(
+            surface_ref.at[:, :, :, pl.ds(c * span, span)], surface[c], load_sems.at[7 + c]
+        )
+        for c in range(pieces)
+    ]
     get_weights = pltpu.make_async_copy(weights_ref, weights, load_sems.at[1])
-    get_surface.start()
     small = [
         pltpu.make_async_copy(src, dst, load_sems.at[3 + n])
         for n, (src, dst) in enumerate(
@@ -260,7 +271,8 @@
             )
         )
     ]
-    for copy in small:
+    get_surface[0].start()
+    for copy in small + get_surface[1:]:
         copy.start()
 
     def remote(src, dst, send, recv, **peer):
@@ -268,46 +280,30 @@
             src_ref=src, dst_ref=dst, send_sem=send, recv_sem=recv,
             device_id=peer, device_id_type=pl.DeviceIdType.MESH,
         )
-
-    barrier = pltpu.get_barrier_semaphore()
-    for k in range(1, owners):
-        pl.semaphore_signal(
-            barrier, inc=1, device_id={"cfd": flip(me, k)}, device_id_type=pl.DeviceIdType.MESH
-        )
-    pl.semaphore_signal(barrier, inc=1, device_id={"ac": 1 - y}, device_id_type=pl.DeviceIdType.MESH)
 
     for copy in small:
         copy.wait()
     flat = flat_normals[...].astype(jnp.float32)
     tall = jnp.concatenate([flat, jnp.zeros((LANES - flat.shape[0], faces), jnp.float32)], axis=0)
     normals[...] = tall.T.reshape(owners, size, LANES)
-    get_surface.wait()
-    get_weights.start()
 
     def wait_all(ref, sem):
         pltpu.make_async_copy(ref, ref, sem).wait()
 
-    def thick_block(place):
-        along = surface[2, place].astype(jnp.float32) * normals[place, :, 0:1]
-        along = along + surface[3, place].astype(jnp.float32) * normals[place, :, 1:2]
-        along = along + surface[4, place].astype(jnp.float32) * normals[place, :, 2:3]
-        return (surface[1, place].astype(jnp.float32) * along).astype(jnp.bfloat16)
-
-    def cut(value, c):
-        return value[:, c * span : (c + 1) * span]
+    def blocks(c, place):
+        along = surface[c][2, place].astype(jnp.float32) * normals[place, :, 0:1]
+        along = along + surface[c][3, place].astype(jnp.float32) * normals[place, :, 1:2]
+        along = along + surface[c][4, place].astype(jnp.float32) * normals[place, :, 2:3]
+        thick = (surface[c][1, place].astype(jnp.float32) * along).astype(jnp.bfloat16)
+        return thick, surface[c][0, place]
 
     order = sorted(range(1, owners), key=lambda k: send_order(k, near))
-    for k in order:
-        place = block_at[flip(me, k)]
-        thick, pressure = thick_block(place), surface[0, place]
-        for c in range(pieces):
-            outgoing[k, c, 0], outgoing[k, c, 1] = cut(thick, c), cut(pressure, c)
-    place = block_at[me]
-    thick, pressure = thick_block(place), surface[0, place]
     for c in range(pieces):
-        arrived[c, me, 0], arrived[c, me, 1] = cut(thick, c), cut(pressure, c)
-    pl.semaphore_wait(barrier, owners)
-    for c in range(pieces):
+        get_surface[c].wait()
+        for k in order:
+            outgoing[k, c, 0], outgoing[k, c, 1] = blocks(c, block_at[flip(me, k)])
+        if c == 0:
+            pl.semaphore_wait(barrier, owners)
         for k in order:
             remote(
                 outgoing.at[k, c],
@@ -316,6 +312,8 @@
                 block_recv.at[c],
                 cfd=flip(me, k),
             ).start()
+        arrived[c, me, 0], arrived[c, me, 1] = blocks(c, block_at[me])
+    get_weights.start()
 
     ids = ids_here[...]
     down = jnp.concatenate([ids, jnp.zeros((LANES - bands, width), jnp.int32)], axis=0).T
@@ -576,7 +574,7 @@
             pltpu.SMEM((owners,), i32),
             pltpu.VMEM((bands, width), i32),
             pltpu.VMEM(area_normals.shape, bf16),
-            pltpu.VMEM((surface_raw.shape[0], owners, size, steps), bf16),
+            [pltpu.VMEM((surface_raw.shape[0], owners, size, span), bf16)] * pieces,
             pltpu.VMEM(kernel_weights.shape, bf16),
             pltpu.VMEM((owners, size, LANES), f32),
             pltpu.VMEM((owners, pieces, 2, size, span), bf16),
@@ -601,7 +599,7 @@
             pltpu.VMEM((2, zs) + tile, bf16),
             pltpu.VMEM((zs, 2) + tile, bf16),
             pltpu.VMEM((zs, 2) + tile, bf16),
-            dma((7,)),
+            dma((7 + pieces,)),
             dma((1,)),
             dma((pieces,)),
             dma((1,)),

time: 38.5 us -> 38.4 us (level)
  no operation moved by 1% of the time
where the time goes in v6:
time: 38.4 us; the launch traced here: 38.2 us
  Pallas kernels  37.6 us (98%)
  other arithmetic  0.67 us (2%)
    pallas_call x1, Pallas kernels, fused(): pl.pallas_call(fused_kernel, out_shape=[jax.ShapeDtypeStruct(tile, f32)]...  37.6 us

profile of v6, /device:TPU:0, one launch (start us, length us, event | category | flops | bytes accessed | tf_op | source)
XLA Modules:
  0.0 38.2 jit_solution(5798374524994153962)
XLA Ops:
  0.0 37.6 %fused.1 = (f32[128,128]{1,0:T(8,128)S(1)}, f32[128,128]{1,0:T(8,128)S(1)}) custom-call(s32[16]{0:T(128)} %lags_ref.1, s32[16]{0:T(128)} %bitcast.3, s32[16,128]{1,0:T(8,128)} %ids_ref.1, bf16[3,128]{1,0:T(4,128)(2,1)} %normals_ref.1, bf16[5,16,8,1024]{3,2,1,0:T(8,128)(2,1)} %bitcast.2, bf16[2,3,2048,128]{3,2,1,0:T(8,128)(2,1)} %weights_ref.1), custom_call_target="tpu_custom_call" | custom-call | tf_op jit(solution)/shard_map/fused/pallas_call | solution.py:567
  37.6 0.7 %pad_maximum_fusion = f32[128,256]{1,0:T(8,128)} fusion(f32[128,128]{1,0:T(8,128)S(1)} %get-tuple-element.8, f32[128,128]{1,0:T(8,128)S(1)} %get-tuple-element.7), kind=kLoop, calls=%fused_computation | loop fusion | flops 32768 | bytes 262144 | tf_op jit(solution)/shard_map/concatenate | solution.py:631

commit v7 on v6

--- a/solution.py
+++ b/solution.py
@@ -83,7 +83,7 @@
             lane < LANES - rest, parts[t], parts[t + 1]
         )
 
-    unroll = 32
+    unroll = 64
 
     @pl.loop(0, width // unroll)
     def _(group):
@@ -398,13 +398,13 @@
                     :, u * LANES : (u + 1) * LANES
                 ].reshape(bands_each, width, LANES)
 
-    @pl.loop(0, bands // 4)
+    @pl.loop(0, bands // 8)
     def _(group):
-        for m in range(4):
-            shift_band(group * 4 + m, half, chunks)
+        for m in range(8):
+            shift_band(group * 8 + m, half, chunks)
 
     get_inverse.wait()
-    unroll = 32
+    unroll = 64
 
     def gather(top, side):
         @pl.loop(0, 2)

time: 38.4 us -> 38.2 us (level)
  no operation moved by 1% of the time
where the time goes in v7:
time: 38.2 us; the launch traced here: 38.1 us
  Pallas kernels  37.4 us (98%)
  other arithmetic  0.67 us (2%)
    pallas_call x1, Pallas kernels, fused(): pl.pallas_call(fused_kernel, out_shape=[jax.ShapeDtypeStruct(tile, f32)]...  37.4 us

profile of v7, /device:TPU:0, one launch (start us, length us, event | category | flops | bytes accessed | tf_op | source)
XLA Modules:
  0.0 38.1 jit_solution(12969347689495791246)
XLA Ops:
  0.0 37.4 %fused.1 = (f32[128,128]{1,0:T(8,128)S(1)}, f32[128,128]{1,0:T(8,128)S(1)}) custom-call(s32[16]{0:T(128)} %lags_ref.1, s32[16]{0:T(128)} %bitcast.3, s32[16,128]{1,0:T(8,128)} %ids_ref.1, bf16[3,128]{1,0:T(4,128)(2,1)} %normals_ref.1, bf16[5,16,8,1024]{3,2,1,0:T(8,128)(2,1)} %bitcast.2, bf16[2,3,2048,128]{3,2,1,0:T(8,128)(2,1)} %weights_ref.1), custom_call_target="tpu_custom_call" | custom-call | tf_op jit(solution)/shard_map/fused/pallas_call | solution.py:567
  37.4 0.7 %pad_maximum_fusion = f32[128,256]{1,0:T(8,128)} fusion(f32[128,128]{1,0:T(8,128)S(1)} %get-tuple-element.8, f32[128,128]{1,0:T(8,128)S(1)} %get-tuple-element.7), kind=kLoop, calls=%fused_computation | loop fusion | flops 32768 | bytes 262144 | tf_op jit(solution)/shard_map/concatenate | solution.py:631

commit v8 on v7

--- a/solution.py
+++ b/solution.py
@@ -546,7 +546,7 @@
 
 def send_order(k, near):
     j = k // near
-    return (0, 3, 1, 2)[j] if j < 4 else j, k
+    return (3, 0, 1, 2)[j] if j < 4 else j, k
 
 
 def fused(surface_raw, area_normals, kernel_weights, block_map, band_observers, band_lags):

time: 38.2 us -> 38.2 us (level)
  no operation moved by 1% of the time
where the time goes in v8:
time: 38.2 us; the launch traced here: 38.1 us
  Pallas kernels  37.4 us (98%)
  other arithmetic  0.67 us (2%)
    pallas_call x1, Pallas kernels, fused(): pl.pallas_call(fused_kernel, out_shape=[jax.ShapeDtypeStruct(tile, f32)]...  37.4 us

profile of v8, /device:TPU:0, one launch (start us, length us, event | category | flops | bytes accessed | tf_op | source)
XLA Modules:
  0.0 38.1 jit_solution(6584238788213934349)
XLA Ops:
  0.0 37.4 %fused.1 = (f32[128,128]{1,0:T(8,128)S(1)}, f32[128,128]{1,0:T(8,128)S(1)}) custom-call(s32[16]{0:T(128)} %lags_ref.1, s32[16]{0:T(128)} %bitcast.3, s32[16,128]{1,0:T(8,128)} %ids_ref.1, bf16[3,128]{1,0:T(4,128)(2,1)} %normals_ref.1, bf16[5,16,8,1024]{3,2,1,0:T(8,128)(2,1)} %bitcast.2, bf16[2,3,2048,128]{3,2,1,0:T(8,128)(2,1)} %weights_ref.1), custom_call_target="tpu_custom_call" | custom-call | tf_op jit(solution)/shard_map/fused/pallas_call | solution.py:567
  37.4 0.7 %pad_maximum_fusion = f32[128,256]{1,0:T(8,128)} fusion(f32[128,128]{1,0:T(8,128)S(1)} %get-tuple-element.8, f32[128,128]{1,0:T(8,128)S(1)} %get-tuple-element.7), kind=kLoop, calls=%fused_computation | loop fusion | flops 32768 | bytes 262144 | tf_op jit(solution)/shard_map/concatenate | solution.py:631
